TPU v7x, 16 devices: a whole 2x2x2 slice. The times are simulated.
16 devices in a mesh: dp: 2 (over z), row: 2 (over y), fsdp: 4 (over x, core).
Axes of the slice: x: 2, y: 2, z: 2, core: 2. Of those that a mesh axis runs over, the one named last changes fastest.
Arguments:
- x_in: bfloat16 [65536, 576], P(('dp', 'row', 'fsdp'))
- dy_out: bfloat16 [65536, 576], P(('dp', 'row', 'fsdp'))
- w_gate: bfloat16 [576, 1536], P(None, ('row', 'fsdp'))
- w_up: bfloat16 [576, 1536], P(None, ('row', 'fsdp'))
- w_down: bfloat16 [1536, 576], P(('row', 'fsdp'))
- g_next: float32 [16, 3, 576, 1536], P(('dp', 'row', 'fsdp'))
Outputs:
- output 1: bfloat16 [65536, 576], P(('dp', 'row', 'fsdp'))
- output 2: float32 [3, 576, 1536], P(None, None, ('row', 'fsdp'))
- output 3: float32 [16, 3, 576, 1536], P(('dp', 'row', 'fsdp'))
All inputs are finite; a program needn't handle non-finite values.
Results may differ from a plain program's by a relative error of at most 0.0121358.
Values are sent between devices in bfloat16 or wider.
A program may use at most 1 GiB of HBM per device.

v0:
```python
import jax
import jax.numpy as jnp
from jax import lax
from jax.sharding import PartitionSpec as P

GROUP_AXES = ("row", "fsdp")
ALL_AXES = ("dp", "row", "fsdp")
CONTRACT_LAST = (((1,), (1,)), ((), ()))
CONTRACT_FIRST = (((0,), (0,)), ((), ()))


def local_backward(x_blk, dy_blk, w_gate, w_up, w_down):
    a_pre = jnp.dot(x_blk, w_gate, preferred_element_type=jnp.float32)
    b_pre = jnp.dot(x_blk, w_up, preferred_element_type=jnp.float32)
    sig_a = jax.nn.sigmoid(a_pre)
    silu_a = a_pre * sig_a
    h_act = (silu_a * b_pre).astype(jnp.bfloat16)
    dh_full = lax.dot_general(dy_blk, w_down, CONTRACT_LAST, preferred_element_type=jnp.float32)
    da_bf = (dh_full * b_pre * sig_a * (1.0 + a_pre * (1.0 - sig_a))).astype(jnp.bfloat16)
    db_bf = (dh_full * silu_a).astype(jnp.bfloat16)
    dx_acc = lax.dot_general(da_bf, w_gate, CONTRACT_LAST, preferred_element_type=jnp.float32) + lax.dot_general(db_bf, w_up, CONTRACT_LAST, preferred_element_type=jnp.float32)
    grad_gate = lax.dot_general(x_blk, da_bf, CONTRACT_FIRST, preferred_element_type=jnp.float32)
    grad_up = lax.dot_general(x_blk, db_bf, CONTRACT_FIRST, preferred_element_type=jnp.float32)
    grad_down = lax.dot_general(dy_blk, h_act, CONTRACT_FIRST, preferred_element_type=jnp.float32)
    return dx_acc.astype(jnp.bfloat16), jnp.stack([grad_gate, grad_up, grad_down])


def solution(mesh):
    def per_device(x_blk, dy_blk, gate_shard, up_shard, down_shard, g_part):
        w_gate = lax.all_gather(gate_shard, GROUP_AXES, axis=1, tiled=True)
        w_up = lax.all_gather(up_shard, GROUP_AXES, axis=1, tiled=True)
        w_down = lax.all_gather(down_shard, GROUP_AXES, axis=0, tiled=True)
        dx_blk, dw_local = local_backward(x_blk, dy_blk, w_gate, w_up, w_down)
        g_summed = lax.psum(g_part[0].astype(jnp.bfloat16), "dp")
        g_shard = lax.psum_scatter(g_summed, GROUP_AXES, scatter_dimension=2, tiled=True)
        return dx_blk, g_shard.astype(jnp.float32), dw_local[None]

    return jax.shard_map(
        per_device,
        mesh=mesh,
        in_specs=(P(ALL_AXES, None), P(ALL_AXES, None), P(None, GROUP_AXES), P(None, GROUP_AXES), P(GROUP_AXES, None), P(ALL_AXES, None, None, None)),
        out_specs=(P(ALL_AXES, None), P(None, None, GROUP_AXES), P(ALL_AXES, None, None, None)),
        check_vma=False,
    )
```

profile of v0, /device:TPU:0, one launch (start us, length us, event | category | flops | bytes accessed | tf_op | source)
XLA Modules:
  0.0 217.3 jit_solution(11736928547460915563)
XLA Ops:
  7.2 0.0 all-gather.6.cloned.1.call-start
  7.2 0.7 all-gather.6.cloned.1.call-update
  7.9 0.0 all-gather.8.cloned.1.call-start
  7.9 0.7 all-gather.8.cloned.1.call-update
  8.6 0.0 all-gather.4.cloned.1.call-start
  8.7 0.7 all-gather.4.cloned.1.call-update
  9.4 0.0 reduce-scatter.2.cloned.1.call-start
  9.4 10.5 %copy.9 = bf16[1,3,576,1536]{2,3,1,0:T(8,128)(2,1)} copy(f32[1,3,576,1536]{3,2,1,0:T(8,128)} %param.11) | data formatting | bytes 15925248 | tf_op args[5]
  19.9 0.0 reduce-scatter.2.cloned.1.call-update
  19.9 0.0 all-reduce.2.cloned.1.call-start
  20.0 15.9 %all-gather.6.cloned.1.call-done = bf16[576,1536]{0,1:T(8,128)(2,1)} async-done(((bf16[576,192]{0,1:T(8,128)(2,1)}), bf16[576,1536]{0,1:T(8,128)(2,1)}) %all-gather.6.cloned.1.call-update) | async-done | bytes 1769488 | tf_op jit(solution)/shard_map/all_gather | solution.py:31
  35.9 17.7 %fusion.5 = f32[4096,1536]{1,0:T(8,128)} fusion(bf16[4096,576]{0,1:T(8,128)(2,1)} %param.6, bf16[576,1536]{0,1:T(8,128)(2,1)} %all-gather.6.cloned.1.call-done), kind=kOutput, calls=%fused_computation.13 | convolution fusion | flops 7247757312 | bytes 31653888 | tf_op jit(solution)/shard_map/dot_general | solution.py:14
  53.6 7.4 %all-gather.8.cloned.1.call-done = bf16[576,1536]{0,1:T(8,128)(2,1)} async-done(((bf16[576,192]{0,1:T(8,128)(2,1)}), bf16[576,1536]{0,1:T(8,128)(2,1)}) %all-gather.8.cloned.1.call-update) | async-done | bytes 1769488 | tf_op jit(solution)/shard_map/all_gather | solution.py:30
  61.0 17.7 %fusion.6 = f32[4096,1536]{1,0:T(8,128)} fusion(bf16[4096,576]{0,1:T(8,128)(2,1)} %param.6, bf16[576,1536]{0,1:T(8,128)(2,1)} %all-gather.8.cloned.1.call-done), kind=kOutput, calls=%fused_computation.14 | convolution fusion | flops 7247757312 | bytes 31653888 | tf_op jit(solution)/shard_map/dot_general | solution.py:13
  78.6 7.4 %all-gather.4.cloned.1.call-done = bf16[1536,576]{1,0:T(8,128)(2,1)} async-done(((bf16[192,576]{1,0:T(8,128)(2,1)}), bf16[1536,576]{1,0:T(8,128)(2,1)}) %all-gather.4.cloned.1.call-update) | async-done | bytes 1769488 | tf_op jit(solution)/shard_map/all_gather | solution.py:32
  86.0 33.1 %multiply_convert_fusion.1 = (bf16[4096,1536]{1,0:T(8,128)(2,1)}, bf16[4096,1536]{1,0:T(8,128)(2,1)}) fusion(f32[4096,1536]{1,0:T(8,128)} %fusion.6, f32[4096,1536]{1,0:T(8,128)} %fusion.5, bf16[4096,576]{0,1:T(8,128)(2,1)} %param.7, bf16[1536,576]{1,0:T(8,128)(2,1)} %all-gather.4.cloned.1.call-done), kind=kOutput, calls=%fused_computation.1 | convolution fusion | flops 7329546240 | bytes 81985536 | tf_op jit(solution)/shard_map/dot_general | solution.py:18
  119.2 0.0 copy-start.2
  119.2 11.6 %convolution_bitcast_fusion = f32[1,576,1536]{2,1,0:T(8,128)S(1)} fusion(bf16[4096,576]{0,1:T(8,128)(2,1)} %param.6, bf16[4096,1536]{1,0:T(8,128)(2,1)} %get-tuple-element.3), kind=kOutput, calls=%fused_computation.10 | convolution fusion | flops 7247757312 | bytes 20840448 | tf_op jit(solution)/shard_map/dot_general | solution.py:23
  130.8 0.0 copy-done.2
  130.8 0.0 copy-start.1
  130.8 13.1 %fusion.7 = f32[4096,576]{0,1:T(8,128)} fusion(bf16[4096,1536]{1,0:T(8,128)(2,1)} %get-tuple-element.4, bf16[576,1536]{0,1:T(8,128)(2,1)S(1)} %copy-done.2), kind=kOutput, calls=%fused_computation.15 | convolution fusion | flops 7247757312 | bytes 23789568 | tf_op jit(solution)/shard_map/dot_general | solution.py:21
  143.9 0.0 copy-done.1
  143.9 13.5 %add_convert_fusion = bf16[4096,576]{0,1:T(8,128)(2,1)} fusion(f32[4096,576]{0,1:T(8,128)} %fusion.7, bf16[4096,1536]{1,0:T(8,128)(2,1)} %get-tuple-element.3, bf16[576,1536]{0,1:T(8,128)(2,1)S(1)} %copy-done.1), kind=kOutput, calls=%fused_computation.7 | convolution fusion | flops 7252475904 | bytes 28508160 | tf_op jit(solution)/shard_map/dot_general | solution.py:21
  157.3 21.6 %fusion.3 = f32[1,576,1536]{2,1,0:T(8,128)} fusion(bf16[4096,576]{0,1:T(8,128)(2,1)} %param.7, f32[4096,1536]{1,0:T(8,128)} %fusion.5, f32[4096,1536]{1,0:T(8,128)} %fusion.6), kind=kOutput, calls=%fused_computation.9 | convolution fusion | flops 7285506048 | bytes 58589184 | tf_op jit(solution)/shard_map/dot_general | solution.py:24
  178.9 0.0 reduce-scatter.2.cloned.1.call-done
  178.9 0.0 all-reduce.2.cloned.1.call-update
  178.9 0.0 copy-start
  178.9 11.6 %convolution_bitcast_fusion.1 = f32[1,576,1536]{2,1,0:T(8,128)S(1)} fusion(bf16[4096,576]{0,1:T(8,128)(2,1)} %param.6, bf16[4096,1536]{1,0:T(8,128)(2,1)} %get-tuple-element.4), kind=kOutput, calls=%fused_computation.11 | convolution fusion | flops 7247757312 | bytes 20840448 | tf_op jit(solution)/shard_map/dot_general | solution.py:22
  190.6 0.0 copy-done
  190.6 5.1 %maximum_bitcast_fusion = f32[1,3,576,1536]{3,2,1,0:T(8,128)} fusion(f32[1,576,1536]{2,1,0:T(8,128)S(1)} %copy-done, f32[1,576,1536]{2,1,0:T(8,128)S(1)} %convolution_bitcast_fusion, f32[1,576,1536]{2,1,0:T(8,128)S(1)} %convolution_bitcast_fusion.1), kind=kLoop, calls=%fused_computation.6 | loop fusion | flops 5308416 | bytes 21233664 | tf_op jit(solution)/shard_map/broadcast_in_dim | solution.py:36
  195.7 12.7 %all-reduce.2.cloned.1.call-done = bf16[3,576,192]{1,2,0:T(8,128)(2,1)} async-done(((bf16[3,576,192]{1,2,0:T(8,128)(2,1)}), bf16[3,576,192]{1,2,0:T(8,128)(2,1)}) %all-reduce.2.cloned.1.call-update) | async-done | bytes 663568 | tf_op jit(solution)/shard_map/psum | solution.py:34
  208.4 2.3 %convert_element_type.26 = f32[3,576,192]{1,2,0:T(8,128)} convert(bf16[3,576,192]{1,2,0:T(8,128)(2,1)} %all-reduce.2.cloned.1.call-done) | non-fusion elementwise | flops 331776 | bytes 1990656 | tf_op jit(solution)/shard_map/convert_element_type | solution.py:36
Async XLA Ops:
  7.2 28.7 %all-gather.6.cloned.1.call-start = ((), (), s32[]{:S(2)}) async-start(), calls=%async_computation.2 | async-start | bytes 2211840 | tf_op jit(solution)/shard_map/all_gather | solution.py:31
  7.9 53.1 %all-gather.8.cloned.1.call-start = ((), (), s32[]{:S(2)}) async-start(), calls=%async_computation.3 | async-start | bytes 2211840 | tf_op jit(solution)/shard_map/all_gather | solution.py:30
  8.6 77.4 %all-gather.4.cloned.1.call-start = ((), (), s32[]{:S(2)}) async-start(), calls=%async_computation.1 | async-start | bytes 2211840 | tf_op jit(solution)/shard_map/all_gather | solution.py:32
  9.4 169.5 %reduce-scatter.2.cloned.1.call-start = ((), (), s32[]{:S(2)}) async-start(), calls=%async_computation.4 | async-start | bytes 6635520 | tf_op jit(solution)/shard_map/reduce_scatter | solution.py:35
  19.9 188.5 %all-reduce.2.cloned.1.call-start = ((), (), s32[]{:S(2)}) async-start(), calls=%async_computation.5 | async-start | bytes 1474560 | tf_op jit(solution)/shard_map/psum | solution.py:34
  119.2 11.6 %copy-start.2 = (bf16[576,1536]{0,1:T(8,128)(2,1)S(1)}, bf16[576,1536]{0,1:T(8,128)(2,1)}, u32[]{:S(2)}) copy-start(bf16[576,1536]{0,1:T(8,128)(2,1)} %all-gather.8.cloned.1.call-done) | copy-start | bytes 5308420
  130.8 13.1 %copy-start.1 = (bf16[576,1536]{0,1:T(8,128)(2,1)S(1)}, bf16[576,1536]{0,1:T(8,128)(2,1)}, u32[]{:S(2)}) copy-start(bf16[576,1536]{0,1:T(8,128)(2,1)} %all-gather.6.cloned.1.call-done) | copy-start | bytes 5308420
  178.9 11.6 %copy-start = (f32[1,576,1536]{2,1,0:T(8,128)S(1)}, f32[1,576,1536]{2,1,0:T(8,128)}, u32[]{:S(2)}) copy-start(f32[1,576,1536]{2,1,0:T(8,128)} %fusion.3) | copy-start | bytes 10616836
Sparse Core Ops, SparseCore 0:
  9.8 26.0 all-gather.5
  37.7 23.1 all-gather.7
  62.8 23.1 all-gather.3
  89.3 53.3 reduce-scatter.1
  179.1 29.3 all-reduce.1
where the time goes:
time: 218 us; the launch traced here: 217 us
  matrix products  140 us (64%)
  waiting for transfers between devices  45.5 us (21%)
  between operations  13.8 us (6%)
  local copies, waits for them, and re-layouts  10.5 us (5%)
  other arithmetic  7.46 us (3%)
    dot_general x1, matrix products, local_backward(): lax.dot_general(dy_blk, w_down, CONTRACT_LAST, preferred_element_type=jnp...  33.1 us
    dot_general x1, matrix products, local_backward(): lax.dot_general(dy_blk, h_act, CONTRACT_FIRST, preferred_element_type=jnp...  21.6 us
    dot_general x1, matrix products, local_backward(): b_pre = jnp.dot(x_blk, w_up, preferred_element_type=jnp.float32)  17.7 us
    dot_general x1, matrix products, local_backward(): a_pre = jnp.dot(x_blk, w_gate, preferred_element_type=jnp.float32)  17.7 us
    all_gather x1, waiting for transfers between devices, per_device(): w_up = lax.all_gather(up_shard, GROUP_AXES, axis=1, tiled=True)  15.9 us
    dot_general x1, matrix products, local_backward(): lax.dot_general(db_bf, w_up, CONTRACT_LAST, preferred_element_type=jnp.fl...  13.5 us
    dot_general x1, matrix products, local_backward(): lax.dot_general(da_bf, w_gate, CONTRACT_LAST, preferred_element_type=jnp....  13.1 us
    psum x1, waiting for transfers between devices, per_device(): g_summed = lax.psum(g_part[0].astype(jnp.bfloat16), 'dp')  12.7 us
  transfers between devices with their start and end apart: 5, of which 4 were waited for; matrix products, arithmetic and copies ran while one was open for 72% of the time, Pallas kernels for 0%

commit v1 on v0

v1 whole, which is shorter than its diff:
```python
import jax
import jax.numpy as jnp
from jax import lax
from jax.experimental import pallas as pl
from jax.experimental.pallas import tpu as pltpu
from jax.sharding import PartitionSpec as P

ALL_AXES = ("dp", "row", "fsdp")
GROUP_AXES = ("row", "fsdp")
MESH = pl.DeviceIdType.MESH
NN = (((1,), (0,)), ((), ()))
NT = (((1,), (1,)), ((), ()))
TN = (((0,), (0,)), ((), ()))
F32 = jnp.float32
BF = jnp.bfloat16
ANY = pl.BlockSpec(memory_space=pl.ANY)

D = 576
H = 1536
T = 4096
TA = 3072
TB = T - TA
CH = 144
BLK = 384
VMEM_LIMIT = 67043328
OWN_OUT, X_OUT, Y_OUT, OWN_MID, X_MID, Y_MID, DIAG = 0, 256, 512, 768, 896, 1024, 1152


def dot(lhs, rhs, dims):
    return lax.dot_general(lhs, rhs, dims, preferred_element_type=F32)


def forward_tile(x, dy, w, rows):
    a = dot(w[0, rows, :], x, NN)
    b = dot(w[1, rows, :], x, NN)
    dh = dot(w[2, rows, :], dy, NN)
    s = jax.nn.sigmoid(a)
    silu = a * s
    h = (silu * b).astype(BF)
    da = (dh * b * s * (1.0 + a * (1.0 - s))).astype(BF)
    db = (dh * silu).astype(BF)
    return h, da, db


def dx_tile(da, db, w, rows):
    return dot(w[0, rows, :], da, TN) + dot(w[1, rows, :], db, TN)


def kernel_a(
    x_hbm, dy_hbm, w1_hbm, w3_hbm, w2_hbm, g_hbm,
    w_out, dw_out, dx_out, sum_out,
    xv, dv, w, da_s, db_s, h_s, dxa, dxo, dwo,
    stage, part, r0, acc, rz, r1, kept, r2, own, theirs,
    in_sem, wl_sem, ws, wr, st_sem, p_s, p_r, z_s, z_r, d1_s, d1_r, d2_s, d2_r, za_s, za_r, f_s, f_r, dxo_sem, dwo_sem, out_sem,
):
    dp = lax.axis_index("dp")
    row = lax.axis_index("row")
    f = lax.axis_index("fsdp")
    c = lax.rem(f, 2)
    x = f // 2
    fx = lax.rem(f + 2, 4)
    to_core = {"fsdp": f + 1 - 2 * c}
    to_x = {"fsdp": fx}
    to_y = {"row": 1 - row}
    to_z = {"dp": 1 - dp}
    to_xy = {"row": row + (1 - c) * (1 - 2 * row), "fsdp": f + c * (fx - f)}
    to_first = {"row": row + c * (1 - 2 * row), "fsdp": f + (1 - c) * (fx - f)}

    out_l, mid_l = 64 * c, 128 * (1 - c)

    def w_load(n):
        i, mid = n // 2, n % 2
        src = (w1_hbm, w3_hbm, w2_hbm)[i]
        if mid:
            return pltpu.make_async_copy(
                src.at[pl.ds(pl.multiple_of(mid_l, 64), 64), :], w.at[i, pl.ds(pl.multiple_of(OWN_MID + 64 * c, 64), 64), :], wl_sem.at[n]
            )
        return pltpu.make_async_copy(
            src.at[pl.ds(pl.multiple_of(out_l, 64), 128), :], w.at[i, pl.ds(pl.multiple_of(OWN_OUT + 128 * c, 128), 128), :], wl_sem.at[n]
        )

    def g_load(k, side):
        half = 1 - dp if k < 3 else dp
        core = c if side == 0 else 1 - c
        rows = pl.ds(pl.multiple_of(864 * core + 432 * half + CH * (k % 3), 16), CH)
        slot = 2 * (k % 3) + side
        return pltpu.make_async_copy(g_hbm.at[rows, :], stage.at[slot], st_sem.at[slot])

    def t_load(t, which):
        src, dst = ((x_hbm, xv), (dy_hbm, dv))[which]
        cols = pl.ds(t * 1024, 1024)
        return pltpu.make_async_copy(src.at[:, cols], dst.at[:, cols], in_sem.at[2 * t + which])

    for n in (0, 2, 4, 1, 3, 5):
        w_load(n).start()
    for k in range(3):
        g_load(k, 1).start()
        g_load(k, 0).start()
        if k == 0:
            t_load(0, 0).start()
            t_load(0, 1).start()
    for t in range(1, TA // 1024):
        t_load(t, 0).start()
        t_load(t, 1).start()

    barrier = pltpu.get_barrier_semaphore()
    for peer in (to_core, to_x, to_y, to_z):
        pl.semaphore_signal(barrier, inc=1, device_id=peer, device_id_type=MESH)
    pl.semaphore_wait(barrier, 4)

    def w_rows(base, size):
        return w.at[:, pl.ds(pl.multiple_of(base, 64), size), :]

    def w_copy(n):
        o, m = 128 * c, 64 * c
        src, dst, size, peer = (
            (OWN_OUT + o, OWN_OUT + o, 128, to_core),
            (OWN_OUT + o, X_OUT + o, 128, to_x),
            (OWN_OUT + o, Y_OUT + o, 128, to_y),
            (OWN_MID + m, OWN_MID + m, 64, to_core),
            (OWN_MID + m, X_MID + m, 64, to_x),
            (OWN_MID + m, Y_MID + m, 64, to_y),
            (X_OUT + o, X_OUT + o, 128, to_core),
            (Y_OUT + o, Y_OUT + o, 128, to_core),
            (X_MID + m, X_MID + m, 64, to_core),
            (Y_MID + m, Y_MID + m, 64, to_core),
            (X_OUT + c * (Y_OUT + 128 - X_OUT), DIAG + 256 * c, 128, to_xy),
            (X_MID + c * (Y_MID + 64 - X_MID), DIAG + 128 + m, 64, to_xy),
            (DIAG + 256 * c, DIAG + 256 * c, 128, to_core),
            (DIAG + 128 + m, DIAG + 128 + m, 64, to_core),
        )[n]
        return pltpu.make_async_remote_copy(
            src_ref=w_rows(src, size), dst_ref=w_rows(dst, size), send_sem=ws.at[n], recv_sem=wr.at[n], device_id=peer, device_id_type=MESH
        )

    def w_send(*ns):
        for n in ns:
            w_copy(n).start()

    def w_arrived(*ns):
        for n in ns:
            w_copy(n).wait_recv()

    def remote(src, dst, s, r, peer):
        return pltpu.make_async_remote_copy(src_ref=src, dst_ref=dst, send_sem=s, recv_sem=r, device_id=peer, device_id_type=MESH)

    def p_copy(k):
        return remote(part.at[k], r0.at[k], p_s.at[k], p_r.at[k], to_core)

    def z_copy(k):
        return remote(acc.at[k], rz.at[k], z_s.at[k], z_r.at[k], to_z)

    def cols(q):
        return pl.ds(pl.multiple_of(q * BLK, BLK), BLK)

    def q_of(j, mine):
        on_x = 2 * j + (x if mine else 1 - x)
        on_y = 2 * (row if mine else 1 - row) + j
        return (1 - c) * on_x + c * on_y

    def d1_copy(k, j):
        return remote(acc.at[3 + k, :, cols(q_of(j, False))], r1.at[k, :, pl.ds(BLK * j, BLK)], d1_s.at[k, j], d1_r.at[k, j], to_first)

    m = (1 - c) * row + c * x

    def d2_copy(k):
        return remote(kept.at[k, :, cols(1 - m)], r2.at[k], d2_s.at[k], d2_r.at[k], to_xy)

    def za_copy(k):
        return remote(own.at[3 * dp + k], own.at[3 * dp + k], za_s.at[k], za_r.at[k], to_z)

    def za_arrival(k):
        return remote(own.at[3 * dp + k], own.at[3 * (1 - dp) + k], za_s.at[k], za_r.at[k], to_z)

    def lanes(core):
        return pl.ds(pl.multiple_of(128 * core, 128), 256)

    f_copy = remote(own.at[:, :, lanes(1 - c)], theirs, f_s, f_r, to_core)
    own_out = pltpu.make_async_copy(own.at[:, :, lanes(c)], sum_out.at[pl.ds(6 * c, 6)], out_sem.at[0])
    their_out = pltpu.make_async_copy(theirs, sum_out.at[pl.ds(6 * (1 - c), 6)], out_sem.at[1])
    w_store = pltpu.make_async_copy(w, w_out, out_sem.at[2])

    def convert(base):
        for k in range(base, base + 3):
            g_load(k, 1).wait()
            part[k] = stage[2 * (k - base) + 1].astype(BF)
            g_load(k, 0).wait()
            acc[k] = stage[2 * (k - base)].astype(BF)
            if k > base:
                p_copy(k - 1).start()
        p_copy(base + 2).start()

    def add_partner(base):
        for k in range(base, base + 3):
            p_copy(k).wait_recv()
            acc[k] = acc[k] + r0[k]

    def z_step(k):
        z_copy(k).wait_recv()
        acc[3 + k] = acc[3 + k] + rz[k]
        d1_copy(k, 0).start()
        d1_copy(k, 1).start()

    def d1_step(k):
        for j in range(2):
            d1_copy(k, j).wait_recv()
        for j in range(2):
            at = pl.ds(BLK * j, BLK)
            kept[k, :, at] = acc[3 + k, :, cols(q_of(j, True))] + r1[k, :, at]
        d2_copy(k).start()

    def d2_step(k):
        d2_copy(k).wait_recv()
        own[3 * dp + k] = kept[k, :, cols(m)] + r2[k]
        za_copy(k).start()

    def dw_copy(slot, i, base):
        return pltpu.make_async_copy(dwo.at[slot], dw_out.at[i, :, pl.ds(pl.multiple_of(base, 256), 256)], dwo_sem.at[slot])

    def dx_copy(t, size):
        at = pl.ds(pl.multiple_of(t * size, size), size)
        return pltpu.make_async_copy(dxo.at[lax.rem(t, 2)], dx_out.at[:, at], dxo_sem.at[lax.rem(t, 2)])

    def f_tile(base, size, t, tile, first, last):
        rows = pl.ds(base, size)
        at = pl.ds(pl.multiple_of(t * tile, tile), tile)
        h, da, db = forward_tile(xv[:, at], dv[:, at], w, rows)
        h_s[:size, at] = h
        da_s[:size, at] = da
        db_s[:size, at] = db
        dx = dx_tile(da, db, w, rows)
        if first:
            dxa[:, at] = dx
        elif last:

            @pl.when(t >= 2)
            def _():
                dx_copy(t - 2, tile).wait()

            dxo[lax.rem(t, 2)] = (dxa[:, at] + dx).astype(BF)
            dx_copy(t, tile).start()
        else:
            dxa[:, at] += dx

    def w_chunk(base, n, i, fresh):
        if not fresh:
            dw_copy(i, i, base + 256 * n - 256).wait()
        at = pl.ds(pl.multiple_of(256 * n, 256), 256)
        lhs = (xv, xv, dv)[i]
        rhs = (da_s, db_s, h_s)[i]
        dwo[i] = dot(lhs[...], rhs[at, :], NT)
        dw_copy(i, i, base + 256 * n).start()

    for n in (0, 2, 4):
        w_load(n).wait()
    w_send(0, 1, 2)
    for n in (1, 3, 5):
        w_load(n).wait()
    w_send(3, 4, 5)
    convert(0)
    for k in range(3, 6):
        g_load(k, 1).start()
        g_load(k, 0).start()
    w_arrived(0)

    @pl.loop(0, TA // 1024)
    def _(t):
        for i in range(TA // 1024):

            @pl.when(t == i)
            def _():
                t_load(i, 0).wait()
                t_load(i, 1).wait()

        @pl.when(t == 1)
        def _():
            convert(3)
            add_partner(0)
            for k in range(3):
                z_copy(k).start()

        f_tile(0, 256, t, 1024, True, False)

    add_partner(3)
    w_chunk(0, 0, 0, True)
    w_chunk(0, 0, 1, True)
    w_arrived(1, 2)
    w_send(6, 7, 10)
    w_chunk(0, 0, 2, True)
    w_arrived(6, 7)

    @pl.loop(0, TA // 1024)
    def _(t):
        @pl.when(t == 2)
        def _():
            w_arrived(3, 4, 5)
            w_send(8, 9, 11)
            z_step(0)

        f_tile(256, 512, t, 1024, False, False)

    d1_step(0)
    for i in range(3):
        dw_copy(i, i, 0).wait()

    @pl.loop(0, 2)
    def _(n):
        @pl.when(n == 1)
        def _():
            d2_step(0)
            w_arrived(10, 11)
            w_send(12, 13)

        for i in range(3):

            @pl.when(n > 0)
            def _():
                dw_copy(i, i, 256 + 256 * n - 256).wait()

            w_chunk(256, n, i, True)

    w_arrived(8, 9, 12, 13)
    w_store.start()
    z_step(1)
    for i in range(3):
        dw_copy(i, i, 512).wait()

    @pl.loop(0, TA // 512)
    def _(t):
        for i, step in enumerate((None, lambda: d1_step(1), lambda: d2_step(1), lambda: z_step(2), lambda: d1_step(2), lambda: d2_step(2))):
            if step is not None:
                pl.when(t == i)(step)
        f_tile(768, 768, t, 512, False, True)

    for k in range(3):
        za_arrival(k).wait_recv()
    f_copy.start()
    own_out.start()

    @pl.loop(0, 3)
    def _(n):
        @pl.when(n == 2)
        def _():
            f_copy.wait_recv()
            their_out.start()

        for i in range(3):

            @pl.when(n > 0)
            def _():
                dw_copy(i, i, 768 + 256 * n - 256).wait()

            w_chunk(768, n, i, True)

    for i in range(3):
        dw_copy(i, i, 1280).wait()
    for t in (TA // 512 - 2, TA // 512 - 1):
        dx_copy(t, 512).wait()
    own_out.wait()
    their_out.wait()
    w_store.wait()
    for n in range(14):
        w_copy(n).wait_send()
    for k in range(6):
        p_copy(k).wait_send()
    for k in range(3):
        z_copy(k).wait_send()
        d1_copy(k, 0).wait_send()
        d1_copy(k, 1).wait_send()
        d2_copy(k).wait_send()
        za_copy(k).wait_send()
    f_copy.wait_send()


def kernel_b(
    x_hbm, dy_hbm, w_hbm, dwp_hbm, dxp_hbm, sum_hbm,
    dx_out, dw_out, dn_out,
    xv, dv, w, dwp, dxp, sums, flip, dn, da_s, db_s, h_s, dxa, dxo, dwo,
    t_sem, w_sem, dwp_sem, misc_sem, dwo_sem, out_sem,
):
    row = lax.axis_index("row")
    f = lax.axis_index("fsdp")
    c = lax.rem(f, 2)
    x = f // 2
    q_own, q_x, q_y, q_d = 2 * row + x, 2 * row + 1 - x, 2 * (1 - row) + x, 2 * (1 - row) + 1 - x
    granule = [3 * q + j for q, j in (
        (q_own, 0), (q_own, 2), (q_x, 0), (q_x, 2), (q_y, 0), (q_y, 2), (q_own, 1), (q_x, 1), (q_y, 1), (q_d, 0), (q_d, 1), (q_d, 2)
    )]

    def t_load(t, which):
        src, dst = ((x_hbm, xv), (dy_hbm, dv))[which]
        return pltpu.make_async_copy(src.at[:, pl.ds(TA + 512 * t, 512)], dst.at[:, pl.ds(512 * t, 512)], t_sem.at[2 * t + which])

    def w_load(g, i):
        rows = pl.ds(768 * g, 768)
        return pltpu.make_async_copy(w_hbm.at[i, rows, :], w.at[i, rows, :], w_sem.at[3 * g + i])

    def dwp_load(g):
        at = pl.ds(768 * g, 768)
        return pltpu.make_async_copy(dwp_hbm.at[:, :, at], dwp.at[:, :, at], dwp_sem.at[g])

    sum_load = pltpu.make_async_copy(sum_hbm, sums, misc_sem.at[0])
    dxp_load = pltpu.make_async_copy(dxp_hbm, dxp, misc_sem.at[1])
    dxp_store = pltpu.make_async_copy(dxp, dx_out.at[:, pl.ds(0, TA)], misc_sem.at[2])
    dx_store = pltpu.make_async_copy(dxo, dx_out.at[:, pl.ds(TA, TB)], out_sem.at[0])
    dn_store = pltpu.make_async_copy(dn, dn_out, out_sem.at[1])

    w_load(0, 0).start()
    t_load(0, 0).start()
    w_load(0, 1).start()
    w_load(0, 2).start()
    t_load(0, 1).start()
    t_load(1, 0).start()
    t_load(1, 1).start()
    sum_load.start()
    dwp_load(0).start()
    for i in range(3):
        w_load(1, i).start()
    dxp_load.start()
    dwp_load(1).start()
    for i in range(3):
        w_load(0, i).wait()

    def dw_copy(g, n, i, part, slot):
        k = 6 * g + part
        where = granule[k]
        for j in (1, 2):
            where = where + jnp.where(n == j, granule[k + 2 * j] - granule[k], 0)
        return pltpu.make_async_copy(
            dwo.at[slot, :, pl.ds(128 * part, 128)], dw_out.at[i, :, pl.ds(pl.multiple_of(128 * where, 128), 128)], dwo_sem.at[slot, part]
        )

    for g in range(2):
        rows = pl.ds(768 * g, 768)
        if g == 1:
            for i in range(3):
                w_load(1, i).wait()

        @pl.loop(0, TB // 512)
        def _(t):
            if g == 0:
                for i in range(TB // 512):

                    @pl.when(t == i)
                    def _():
                        t_load(i, 0).wait()
                        t_load(i, 1).wait()

            at = pl.ds(pl.multiple_of(t * 512, 512), 512)
            h, da, db = forward_tile(xv[:, at], dv[:, at], w, rows)
            h_s[:, at] = h
            da_s[:, at] = da
            db_s[:, at] = db
            dx = dx_tile(da, db, w, rows)
            if g == 0:
                dxa[:, at] = dx
            else:
                dxo[:, at] = (dxa[:, at] + dx).astype(BF)

        if g == 0:
            sum_load.wait()
            for i in range(3):
                flip[...] = jnp.transpose(sums[pl.ds(576 * i, 576), :].astype(F32))
                dn[i] = flip[pl.ds(pl.multiple_of(64 * c, 64), 192), :]
            dn_store.start()
        else:
            dx_store.start()
            dxp_load.wait()
            dxp_store.start()
        dwp_load(g).wait()

        @pl.loop(0, 3)
        def _(n):
            for i in range(3):
                for part in range(2):

                    @pl.when(n > 0)
                    def _():
                        dw_copy(g, n - 1, i, part, i).wait()

                    if g == 1:

                        @pl.when(n == 0)
                        def _():
                            dw_copy(0, 2, i, part, i).wait()

                cut = pl.ds(pl.multiple_of(256 * n, 256), 256)
                at = pl.ds(pl.multiple_of(768 * g + 256 * n, 256), 256)
                lhs = (xv, xv, dv)[i]
                rhs = (da_s, db_s, h_s)[i]
                dwo[i] = dwp[i, :, at] + dot(lhs[...], rhs[cut, :], NT)
                for part in range(2):
                    dw_copy(g, n, i, part, i).start()

    for i in range(3):
        for part in range(2):
            dw_copy(1, 2, i, part, i).wait()
    dx_store.wait()
    dxp_store.wait()
    dn_store.wait()


def per_device(x_blk, dy_blk, gate_shard, up_shard, down_shard, g_part):
    x_t, dy_t = x_blk.T, dy_blk.T
    dma = pltpu.SemaphoreType.DMA
    vm = pltpu.VMEM
    shape = jax.ShapeDtypeStruct
    w_all, dw_part, dx_part, sums = pl.pallas_call(
        kernel_a,
        out_shape=(shape((3, H, D), BF), shape((3, D, H), F32), shape((D, TA), BF), shape((12, CH, 256), BF)),
        in_specs=[ANY] * 6,
        out_specs=(ANY,) * 4,
        scratch_shapes=[
            vm((D, TA), BF), vm((D, TA), BF), vm((3, H, D), BF), vm((768, TA), BF), vm((768, TA), BF), vm((768, TA), BF),
            vm((D, TA), F32), vm((2, D, 512), BF), vm((3, D, 256), F32),
            vm((6, CH, H), F32), vm((6, CH, H), BF), vm((6, CH, H), BF), vm((6, CH, H), BF), vm((3, CH, H), BF),
            vm((3, CH, 2 * BLK), BF), vm((3, CH, 2 * BLK), BF), vm((3, CH, BLK), BF), vm((6, CH, BLK), BF), vm((6, CH, 256), BF),
            dma((TA // 512,)), dma((6,)), dma((14,)), dma((14,)), dma((6,)), dma((6,)), dma((6,)), dma((3,)), dma((3,)),
            dma((3, 2)), dma((3, 2)), dma((3,)), dma((3,)), dma((3,)), dma((3,)), dma, dma, dma((2,)), dma((3,)), dma((3,)),
        ],
        compiler_params=pltpu.CompilerParams(collective_id=0, has_side_effects=True, vmem_limit_bytes=VMEM_LIMIT),
        name="gather_reduce_backward",
    )(x_t, dy_t, gate_shard.T, up_shard.T, down_shard, g_part.reshape(3 * D, H))
    dx_t, dw_local, dn_t = pl.pallas_call(
        kernel_b,
        out_shape=(shape((D, T), BF), shape((3, D, H), F32), shape((3, 192, D), F32)),
        in_specs=[ANY] * 6,
        out_specs=(ANY,) * 3,
        scratch_shapes=[
            vm((D, TB), BF), vm((D, TB), BF), vm((3, H, D), BF), vm((3, D, H), F32), vm((D, TA), BF), vm((3 * D, 256), BF),
            vm((256, D), F32), vm((3, 192, D), F32), vm((768, TB), BF), vm((768, TB), BF), vm((768, TB), BF),
            vm((D, TB), F32), vm((D, TB), BF), vm((3, D, 256), F32),
            dma((TB // 256,)), dma((6,)), dma((2,)), dma((3,)), dma((3, 2)), dma((2,)),
        ],
        compiler_params=pltpu.CompilerParams(vmem_limit_bytes=VMEM_LIMIT),
        name="finish_backward",
    )(x_t, dy_t, w_all, dw_part, dx_part, sums.reshape(3 * D, 256))
    return dx_t.T, jnp.swapaxes(dn_t, 1, 2), dw_local[None]


def solution(mesh):
    return jax.shard_map(
        per_device,
        mesh=mesh,
        in_specs=(P(ALL_AXES, None), P(ALL_AXES, None), P(None, GROUP_AXES), P(None, GROUP_AXES), P(GROUP_AXES, None), P(ALL_AXES, None, None, None)),
        out_specs=(P(ALL_AXES, None), P(None, None, GROUP_AXES), P(ALL_AXES, None, None, None)),
        check_vma=False,
    )
```

time: 218 us -> 120 us (0.55)
  matrix products: 140 us -> 0 us
  Pallas kernels: 0 us -> 119 us
  waiting for transfers between devices: 45.5 us -> 0 us
  between operations: 13.8 us -> 0.8 us
  local copies, waits for them, and re-layouts: 10.5 us -> 0 us
  other arithmetic: 7.46 us -> 0 us
    dot_general x8 -> x0, matrix products: 140 us -> none  [the longest x1 33.1 us: local_backward(): lax.dot_general(dy_blk, w_down, CONTRACT_LAST, preferred_element_type=jnp...]
    pallas_call x0 -> x2, Pallas kernels: none -> 119 us  [the longest x1 89 us: per_device(): pl.pallas_call(kernel_a, out_shape=(shape((3, H, D), BF), shape((3, D, H)...]
    all_gather x3 -> x0, waiting for transfers between devices: 30.7 us -> none  [the longest x1 15.9 us: per_device(): w_up = lax.all_gather(up_shard, GROUP_AXES, axis=1, tiled=True)]
    psum x1 -> x0, waiting for transfers between devices: 12.7 us -> none  [per_device(): g_summed = lax.psum(g_part[0].astype(jnp.bfloat16), 'dp')]
    unnamed x7 -> x0, local copies, waits for them, and re-layouts: 10.5 us -> none
    broadcast_in_dim x1 -> x0, other arithmetic: 5.13 us -> none  [per_device(): return (dx_blk, g_shard.astype(jnp.float32), dw_local[None])]
    convert_element_type x1 -> x0, other arithmetic: 2.33 us -> none  [per_device(): return (dx_blk, g_shard.astype(jnp.float32), dw_local[None])]
  transfers between devices with their start and end apart: 5 -> 0, of which waited for: 4 -> 0; matrix products, arithmetic and copies ran while one was open for 72% -> 0% of each run, Pallas kernels for 0% -> 0%
where the time goes in v1:
time: 120 us
  Pallas kernels  119 us (99%)
    pallas_call x1, Pallas kernels, per_device(): pl.pallas_call(kernel_a, out_shape=(shape((3, H, D), BF), shape((3, D, H)...  89 us
    pallas_call x1, Pallas kernels, per_device(): pl.pallas_call(kernel_b, out_shape=(shape((D, T), BF), shape((3, D, H), F...  29.7 us

profile of v1, /device:TPU:0, one launch (start us, length us, event | category | flops | bytes accessed | tf_op | source)
XLA Modules:
  0.0 119.5 jit_solution(456931623796158736)
XLA Ops:
  0.6 89.0 %gather_reduce_backward.1 = (bf16[3,1536,576]{2,1,0:T(8,128)(2,1)}, f32[3,576,1536]{2,1,0:T(8,128)}, bf16[576,3072]{1,0:T(8,128)(2,1)}, bf16[12,144,256]{2,1,0:T(8,128)(2,1)}) custom-call(bf16[576,4096]{1,0:T(8,128)(2,1)} %bitcast.9, bf16[576,4096]{1,0:T(8,128)(2,1)} %bitcast.11, bf16[192,576]{1,0:T(8,128)(2,1)} %bitcast.15, bf16[192,576]{1,0:T(8,128)(2,1)} %bitcast.16, ...), custom_call_target="tpu_custom_call" | custom-call | tf_op jit(solution)/shard_map/gather_reduce_backward/pallas_call | solution.py:508
  89.6 29.7 %finish_backward.1 = (bf16[576,4096]{1,0:T(8,128)(2,1)}, f32[3,576,1536]{2,1,0:T(8,128)}, f32[3,192,576]{2,1,0:T(8,128)}) custom-call(bf16[576,4096]{1,0:T(8,128)(2,1)} %bitcast.10, bf16[576,4096]{1,0:T(8,128)(2,1)} %bitcast.12, bf16[3,1536,576]{2,1,0:T(8,128)(2,1)} %get-tuple-element.10.w_hbm, f32[3,576,1536]{2,1,0:T(8,128)} %get-tuple-element.11.dwp_hbm, ...), custom_call_target="tpu_custom_call" | custom-call | tf_op jit(solution)/shard_map/finish_backward/pallas_call | solution.py:524

commit v2 on v1

--- a/solution.py
+++ b/solution.py
@@ -49,7 +49,7 @@
 def kernel_a(
     x_hbm, dy_hbm, w1_hbm, w3_hbm, w2_hbm, g_hbm,
     w_out, dw_out, dx_out, sum_out,
-    xv, dv, w, da_s, db_s, h_s, dxa, dxo, dwo,
+    xv, dv, w, da_s, db_s, h_s, dxa, dxo, dwa,
     stage, part, r0, acc, rz, r1, kept, r2, own, theirs,
     in_sem, wl_sem, ws, wr, st_sem, p_s, p_r, z_s, z_r, d1_s, d1_r, d2_s, d2_r, za_s, za_r, f_s, f_r, dxo_sem, dwo_sem, out_sem,
 ):
@@ -106,6 +106,8 @@
     barrier = pltpu.get_barrier_semaphore()
     for peer in (to_core, to_x, to_y, to_z):
         pl.semaphore_signal(barrier, inc=1, device_id=peer, device_id_type=MESH)
+    for i in range(3):
+        dwa[i] = jnp.zeros((D, H), F32)
     pl.semaphore_wait(barrier, 4)
 
     def w_rows(base, size):
@@ -214,42 +216,30 @@
         own[3 * dp + k] = kept[k, :, cols(m)] + r2[k]
         za_copy(k).start()
 
-    def dw_copy(slot, i, base):
-        return pltpu.make_async_copy(dwo.at[slot], dw_out.at[i, :, pl.ds(pl.multiple_of(base, 256), 256)], dwo_sem.at[slot])
+    def dw_copy(n, base, size):
+        at = pl.ds(base, size)
+        return pltpu.make_async_copy(dwa.at[:, :, at], dw_out.at[:, :, at], dwo_sem.at[n])
 
     def dx_copy(t, size):
         at = pl.ds(pl.multiple_of(t * size, size), size)
         return pltpu.make_async_copy(dxo.at[lax.rem(t, 2)], dx_out.at[:, at], dxo_sem.at[lax.rem(t, 2)])
 
-    def f_tile(base, size, t, tile, first, last):
+    def tile_step(base, size, t, tile, first, last):
         rows = pl.ds(base, size)
         at = pl.ds(pl.multiple_of(t * tile, tile), tile)
-        h, da, db = forward_tile(xv[:, at], dv[:, at], w, rows)
-        h_s[:size, at] = h
-        da_s[:size, at] = da
-        db_s[:size, at] = db
+        xt, dyt = xv[:, at], dv[:, at]
+        h_s[:size, :tile], da_s[:size, :tile], db_s[:size, :tile] = forward_tile(xt, dyt, w, rows)
+        h, da, db = h_s[:size, :tile], da_s[:size, :tile], db_s[:size, :tile]
         dx = dx_tile(da, db, w, rows)
         if first:
             dxa[:, at] = dx
         elif last:
-
-            @pl.when(t >= 2)
-            def _():
-                dx_copy(t - 2, tile).wait()
-
             dxo[lax.rem(t, 2)] = (dxa[:, at] + dx).astype(BF)
-            dx_copy(t, tile).start()
         else:
             dxa[:, at] += dx
-
-    def w_chunk(base, n, i, fresh):
-        if not fresh:
-            dw_copy(i, i, base + 256 * n - 256).wait()
-        at = pl.ds(pl.multiple_of(256 * n, 256), 256)
-        lhs = (xv, xv, dv)[i]
-        rhs = (da_s, db_s, h_s)[i]
-        dwo[i] = dot(lhs[...], rhs[at, :], NT)
-        dw_copy(i, i, base + 256 * n).start()
+        dwa[0, :, rows] += dot(xt, da, NT)
+        dwa[1, :, rows] += dot(xt, db, NT)
+        dwa[2, :, rows] += dot(dyt, h, NT)
 
     for n in (0, 2, 4):
         w_load(n).wait()
@@ -279,81 +269,61 @@
             for k in range(3):
                 z_copy(k).start()
 
-        f_tile(0, 256, t, 1024, True, False)
-
-    add_partner(3)
-    w_chunk(0, 0, 0, True)
-    w_chunk(0, 0, 1, True)
+        tile_step(0, 256, t, 1024, True, False)
+
+    dw_copy(0, 0, 256).start()
     w_arrived(1, 2)
     w_send(6, 7, 10)
-    w_chunk(0, 0, 2, True)
+    add_partner(3)
     w_arrived(6, 7)
 
     @pl.loop(0, TA // 1024)
     def _(t):
-        @pl.when(t == 2)
+        @pl.when(t == 1)
         def _():
             w_arrived(3, 4, 5)
             w_send(8, 9, 11)
             z_step(0)
 
-        f_tile(256, 512, t, 1024, False, False)
-
-    d1_step(0)
-    for i in range(3):
-        dw_copy(i, i, 0).wait()
-
-    @pl.loop(0, 2)
-    def _(n):
-        @pl.when(n == 1)
+        @pl.when(t == 2)
         def _():
-            d2_step(0)
             w_arrived(10, 11)
             w_send(12, 13)
-
-        for i in range(3):
-
-            @pl.when(n > 0)
-            def _():
-                dw_copy(i, i, 256 + 256 * n - 256).wait()
-
-            w_chunk(256, n, i, True)
-
+            d1_step(0)
+
+        tile_step(256, 512, t, 1024, False, False)
+
+    dw_copy(1, 256, 512).start()
+    d2_step(0)
     w_arrived(8, 9, 12, 13)
     w_store.start()
-    z_step(1)
-    for i in range(3):
-        dw_copy(i, i, 512).wait()
+
+    def g_output():
+        for k in range(3):
+            za_arrival(k).wait_recv()
+        f_copy.start()
+        own_out.start()
+
+    def z2_d21():
+        z_step(2)
+        d2_step(1)
 
     @pl.loop(0, TA // 512)
     def _(t):
-        for i, step in enumerate((None, lambda: d1_step(1), lambda: d2_step(1), lambda: z_step(2), lambda: d1_step(2), lambda: d2_step(2))):
-            if step is not None:
-                pl.when(t == i)(step)
-        f_tile(768, 768, t, 512, False, True)
-
-    for k in range(3):
-        za_arrival(k).wait_recv()
-    f_copy.start()
-    own_out.start()
-
-    @pl.loop(0, 3)
-    def _(n):
-        @pl.when(n == 2)
+        steps = (lambda: z_step(1), lambda: d1_step(1), z2_d21, lambda: d1_step(2), lambda: d2_step(2), g_output)
+        for i, step in enumerate(steps):
+            pl.when(t == i)(step)
+
+        @pl.when(t >= 2)
         def _():
-            f_copy.wait_recv()
-            their_out.start()
-
-        for i in range(3):
-
-            @pl.when(n > 0)
-            def _():
-                dw_copy(i, i, 768 + 256 * n - 256).wait()
-
-            w_chunk(768, n, i, True)
-
-    for i in range(3):
-        dw_copy(i, i, 1280).wait()
+            dx_copy(t - 2, 512).wait()
+
+        tile_step(768, 768, t, 512, False, True)
+        dx_copy(t, 512).start()
+
+    dw_copy(2, 768, 768).start()
+    f_copy.wait_recv()
+    their_out.start()
     for t in (TA // 512 - 2, TA // 512 - 1):
         dx_copy(t, 512).wait()
     own_out.wait()
@@ -370,12 +340,15 @@
         d2_copy(k).wait_send()
         za_copy(k).wait_send()
     f_copy.wait_send()
+    dw_copy(0, 0, 256).wait()
+    dw_copy(1, 256, 512).wait()
+    dw_copy(2, 768, 768).wait()
 
 
 def kernel_b(
     x_hbm, dy_hbm, w_hbm, dwp_hbm, dxp_hbm, sum_hbm,
     dx_out, dw_out, dn_out,
-    xv, dv, w, dwp, dxp, sums, flip, dn, da_s, db_s, h_s, dxa, dxo, dwo,
+    xv, dv, w, dwa, dxp, sums, flip, dn, da_s, db_s, h_s, dxa, dxo,
     t_sem, w_sem, dwp_sem, misc_sem, dwo_sem, out_sem,
 ):
     row = lax.axis_index("row")
@@ -397,7 +370,7 @@
 
     def dwp_load(g):
         at = pl.ds(768 * g, 768)
-        return pltpu.make_async_copy(dwp_hbm.at[:, :, at], dwp.at[:, :, at], dwp_sem.at[g])
+        return pltpu.make_async_copy(dwp_hbm.at[:, :, at], dwa.at[:, :, at], dwp_sem.at[g])
 
     sum_load = pltpu.make_async_copy(sum_hbm, sums, misc_sem.at[0])
     dxp_load = pltpu.make_async_copy(dxp_hbm, dxp, misc_sem.at[1])
@@ -421,80 +394,53 @@
     for i in range(3):
         w_load(0, i).wait()
 
-    def dw_copy(g, n, i, part, slot):
-        k = 6 * g + part
-        where = granule[k]
-        for j in (1, 2):
-            where = where + jnp.where(n == j, granule[k + 2 * j] - granule[k], 0)
-        return pltpu.make_async_copy(
-            dwo.at[slot, :, pl.ds(128 * part, 128)], dw_out.at[i, :, pl.ds(pl.multiple_of(128 * where, 128), 128)], dwo_sem.at[slot, part]
-        )
-
-    for g in range(2):
+    def dw_copy(k):
+        at = pl.ds(pl.multiple_of(128 * granule[k], 128), 128)
+        return pltpu.make_async_copy(dwa.at[:, :, pl.ds(128 * k, 128)], dw_out.at[:, :, at], dwo_sem.at[k])
+
+    def tile_step(g, t, between):
         rows = pl.ds(768 * g, 768)
-        if g == 1:
-            for i in range(3):
-                w_load(1, i).wait()
-
-        @pl.loop(0, TB // 512)
-        def _(t):
-            if g == 0:
-                for i in range(TB // 512):
-
-                    @pl.when(t == i)
-                    def _():
-                        t_load(i, 0).wait()
-                        t_load(i, 1).wait()
-
-            at = pl.ds(pl.multiple_of(t * 512, 512), 512)
-            h, da, db = forward_tile(xv[:, at], dv[:, at], w, rows)
-            h_s[:, at] = h
-            da_s[:, at] = da
-            db_s[:, at] = db
-            dx = dx_tile(da, db, w, rows)
-            if g == 0:
-                dxa[:, at] = dx
-            else:
-                dxo[:, at] = (dxa[:, at] + dx).astype(BF)
-
+        at = pl.ds(pl.multiple_of(t * 512, 512), 512)
+        xt, dyt = xv[:, at], dv[:, at]
+        h_s[...], da_s[...], db_s[...] = forward_tile(xt, dyt, w, rows)
+        h, da, db = h_s[...], da_s[...], db_s[...]
+        dx = dx_tile(da, db, w, rows)
         if g == 0:
-            sum_load.wait()
-            for i in range(3):
-                flip[...] = jnp.transpose(sums[pl.ds(576 * i, 576), :].astype(F32))
-                dn[i] = flip[pl.ds(pl.multiple_of(64 * c, 64), 192), :]
-            dn_store.start()
+            dxa[:, at] = dx
         else:
-            dx_store.start()
-            dxp_load.wait()
-            dxp_store.start()
-        dwp_load(g).wait()
-
-        @pl.loop(0, 3)
-        def _(n):
-            for i in range(3):
-                for part in range(2):
-
-                    @pl.when(n > 0)
-                    def _():
-                        dw_copy(g, n - 1, i, part, i).wait()
-
-                    if g == 1:
-
-                        @pl.when(n == 0)
-                        def _():
-                            dw_copy(0, 2, i, part, i).wait()
-
-                cut = pl.ds(pl.multiple_of(256 * n, 256), 256)
-                at = pl.ds(pl.multiple_of(768 * g + 256 * n, 256), 256)
-                lhs = (xv, xv, dv)[i]
-                rhs = (da_s, db_s, h_s)[i]
-                dwo[i] = dwp[i, :, at] + dot(lhs[...], rhs[cut, :], NT)
-                for part in range(2):
-                    dw_copy(g, n, i, part, i).start()
-
+            dxo[:, at] = (dxa[:, at] + dx).astype(BF)
+        if between is not None:
+            between()
+        dwa[0, :, rows] += dot(xt, da, NT)
+        dwa[1, :, rows] += dot(xt, db, NT)
+        dwa[2, :, rows] += dot(dyt, h, NT)
+
+    for t in range(2):
+        for which in range(2):
+            t_load(t, which).wait()
+        tile_step(0, t, dwp_load(0).wait if t == 0 else None)
+    for k in range(6):
+        dw_copy(k).start()
+    sum_load.wait()
     for i in range(3):
-        for part in range(2):
-            dw_copy(1, 2, i, part, i).wait()
+        flip[...] = jnp.transpose(sums[pl.ds(576 * i, 576), :].astype(F32))
+        dn[i] = flip[pl.ds(pl.multiple_of(64 * c, 64), 192), :]
+    dn_store.start()
+    for i in range(3):
+        w_load(1, i).wait()
+    dxp_load.wait()
+    dxp_store.start()
+    dwp_load(1).wait()
+
+    @pl.loop(0, TB // 512)
+    def _(t):
+        tile_step(1, t, None)
+
+    for k in range(6, 12):
+        dw_copy(k).start()
+    dx_store.start()
+    for k in range(12):
+        dw_copy(k).wait()
     dx_store.wait()
     dxp_store.wait()
     dn_store.wait()
@@ -511,8 +457,8 @@
         in_specs=[ANY] * 6,
         out_specs=(ANY,) * 4,
         scratch_shapes=[
-            vm((D, TA), BF), vm((D, TA), BF), vm((3, H, D), BF), vm((768, TA), BF), vm((768, TA), BF), vm((768, TA), BF),
-            vm((D, TA), F32), vm((2, D, 512), BF), vm((3, D, 256), F32),
+            vm((D, TA), BF), vm((D, TA), BF), vm((3, H, D), BF), vm((768, 1024), BF), vm((768, 1024), BF), vm((768, 1024), BF),
+            vm((D, TA), F32), vm((2, D, 512), BF), vm((3, D, H), F32),
             vm((6, CH, H), F32), vm((6, CH, H), BF), vm((6, CH, H), BF), vm((6, CH, H), BF), vm((3, CH, H), BF),
             vm((3, CH, 2 * BLK), BF), vm((3, CH, 2 * BLK), BF), vm((3, CH, BLK), BF), vm((6, CH, BLK), BF), vm((6, CH, 256), BF),
             dma((TA // 512,)), dma((6,)), dma((14,)), dma((14,)), dma((6,)), dma((6,)), dma((6,)), dma((3,)), dma((3,)),
@@ -528,9 +474,9 @@
         out_specs=(ANY,) * 3,
         scratch_shapes=[
             vm((D, TB), BF), vm((D, TB), BF), vm((3, H, D), BF), vm((3, D, H), F32), vm((D, TA), BF), vm((3 * D, 256), BF),
-            vm((256, D), F32), vm((3, 192, D), F32), vm((768, TB), BF), vm((768, TB), BF), vm((768, TB), BF),
-            vm((D, TB), F32), vm((D, TB), BF), vm((3, D, 256), F32),
-            dma((TB // 256,)), dma((6,)), dma((2,)), dma((3,)), dma((3, 2)), dma((2,)),
+            vm((256, D), F32), vm((3, 192, D), F32), vm((768, 512), BF), vm((768, 512), BF), vm((768, 512), BF),
+            vm((D, TB), F32), vm((D, TB), BF),
+            dma((TB // 256,)), dma((6,)), dma((2,)), dma((3,)), dma((12,)), dma((2,)),
         ],
         compiler_params=pltpu.CompilerParams(vmem_limit_bytes=VMEM_LIMIT),
         name="finish_backward",

time: 120 us -> 96 us (0.80)
  Pallas kernels: 119 us -> 95 us
    pallas_call x1, Pallas kernels: 89 us -> 70.2 us  [per_device(): pl.pallas_call(kernel_a, out_shape=(shape((3, H, D), BF), shape((3, D, H)...]
    pallas_call x1, Pallas kernels: 29.7 us -> 24.8 us  [per_device(): pl.pallas_call(kernel_b, out_shape=(shape((D, T), BF), shape((3, D, H), F...]
where the time goes in v2:
time: 96 us; the launch traced here: 95.9 us
  Pallas kernels  95 us (99%)
    pallas_call x1, Pallas kernels, per_device(): pl.pallas_call(kernel_a, out_shape=(shape((3, H, D), BF), shape((3, D, H)...  70.2 us
    pallas_call x1, Pallas kernels, per_device(): pl.pallas_call(kernel_b, out_shape=(shape((D, T), BF), shape((3, D, H), F...  24.8 us

profile of v2, /device:TPU:0, one launch (start us, length us, event | category | flops | bytes accessed | tf_op | source)
XLA Modules:
  0.0 95.9 jit_solution(7315503049523896603)
XLA Ops:
  0.6 70.2 %gather_reduce_backward.1 = (bf16[3,1536,576]{2,1,0:T(8,128)(2,1)}, f32[3,576,1536]{2,1,0:T(8,128)}, bf16[576,3072]{1,0:T(8,128)(2,1)}, bf16[12,144,256]{2,1,0:T(8,128)(2,1)}) custom-call(bf16[576,4096]{1,0:T(8,128)(2,1)} %bitcast.9, bf16[576,4096]{1,0:T(8,128)(2,1)} %bitcast.11, bf16[192,576]{1,0:T(8,128)(2,1)} %bitcast.15, bf16[192,576]{1,0:T(8,128)(2,1)} %bitcast.16, ...), custom_call_target="tpu_custom_call" | custom-call | tf_op jit(solution)/shard_map/gather_reduce_backward/pallas_call | solution.py:454
  70.9 24.8 %finish_backward.1 = (bf16[576,4096]{1,0:T(8,128)(2,1)}, f32[3,576,1536]{2,1,0:T(8,128)}, f32[3,192,576]{2,1,0:T(8,128)}) custom-call(bf16[576,4096]{1,0:T(8,128)(2,1)} %bitcast.10, bf16[576,4096]{1,0:T(8,128)(2,1)} %bitcast.12, bf16[3,1536,576]{2,1,0:T(8,128)(2,1)} %get-tuple-element.10.w_hbm, f32[3,576,1536]{2,1,0:T(8,128)} %get-tuple-element.11.dwp_hbm, ...), custom_call_target="tpu_custom_call" | custom-call | tf_op jit(solution)/shard_map/finish_backward/pallas_call | solution.py:470

commit v3 on v2

--- a/solution.py
+++ b/solution.py
@@ -14,6 +14,7 @@
 F32 = jnp.float32
 BF = jnp.bfloat16
 ANY = pl.BlockSpec(memory_space=pl.ANY)
+VM = pl.BlockSpec(memory_space=pltpu.VMEM)
 
 D = 576
 H = 1536
@@ -23,6 +24,8 @@
 CH = 144
 BLK = 384
 VMEM_LIMIT = 67043328
+VMEM_A = 47 * 2**20
+VMEM_B = 46 * 2**20
 OWN_OUT, X_OUT, Y_OUT, OWN_MID, X_MID, Y_MID, DIAG = 0, 256, 512, 768, 896, 1024, 1152
 
 
@@ -48,8 +51,8 @@
 
 def kernel_a(
     x_hbm, dy_hbm, w1_hbm, w3_hbm, w2_hbm, g_hbm,
-    w_out, dw_out, dx_out, sum_out,
-    xv, dv, w, da_s, db_s, h_s, dxa, dxo, dwa,
+    w, dwa, dx_out, sum_out,
+    xv, dv, da_s, db_s, h_s, dxa, dxo,
     stage, part, r0, acc, rz, r1, kept, r2, own, theirs,
     in_sem, wl_sem, ws, wr, st_sem, p_s, p_r, z_s, z_r, d1_s, d1_r, d2_s, d2_r, za_s, za_r, f_s, f_r, dxo_sem, dwo_sem, out_sem,
 ):
@@ -180,7 +183,6 @@
     f_copy = remote(own.at[:, :, lanes(1 - c)], theirs, f_s, f_r, to_core)
     own_out = pltpu.make_async_copy(own.at[:, :, lanes(c)], sum_out.at[pl.ds(6 * c, 6)], out_sem.at[0])
     their_out = pltpu.make_async_copy(theirs, sum_out.at[pl.ds(6 * (1 - c), 6)], out_sem.at[1])
-    w_store = pltpu.make_async_copy(w, w_out, out_sem.at[2])
 
     def convert(base):
         for k in range(base, base + 3):
@@ -215,10 +217,6 @@
         d2_copy(k).wait_recv()
         own[3 * dp + k] = kept[k, :, cols(m)] + r2[k]
         za_copy(k).start()
-
-    def dw_copy(n, base, size):
-        at = pl.ds(base, size)
-        return pltpu.make_async_copy(dwa.at[:, :, at], dw_out.at[:, :, at], dwo_sem.at[n])
 
     def dx_copy(t, size):
         at = pl.ds(pl.multiple_of(t * size, size), size)
@@ -271,7 +269,6 @@
 
         tile_step(0, 256, t, 1024, True, False)
 
-    dw_copy(0, 0, 256).start()
     w_arrived(1, 2)
     w_send(6, 7, 10)
     add_partner(3)
@@ -293,10 +290,8 @@
 
         tile_step(256, 512, t, 1024, False, False)
 
-    dw_copy(1, 256, 512).start()
     d2_step(0)
     w_arrived(8, 9, 12, 13)
-    w_store.start()
 
     def g_output():
         for k in range(3):
@@ -321,14 +316,12 @@
         tile_step(768, 768, t, 512, False, True)
         dx_copy(t, 512).start()
 
-    dw_copy(2, 768, 768).start()
     f_copy.wait_recv()
     their_out.start()
     for t in (TA // 512 - 2, TA // 512 - 1):
         dx_copy(t, 512).wait()
     own_out.wait()
     their_out.wait()
-    w_store.wait()
     for n in range(14):
         w_copy(n).wait_send()
     for k in range(6):
@@ -340,16 +333,13 @@
         d2_copy(k).wait_send()
         za_copy(k).wait_send()
     f_copy.wait_send()
-    dw_copy(0, 0, 256).wait()
-    dw_copy(1, 256, 512).wait()
-    dw_copy(2, 768, 768).wait()
 
 
 def kernel_b(
-    x_hbm, dy_hbm, w_hbm, dwp_hbm, dxp_hbm, sum_hbm,
+    x_hbm, dy_hbm, w, dwp, dxp_hbm, sum_hbm,
     dx_out, dw_out, dn_out,
-    xv, dv, w, dwa, dxp, sums, flip, dn, da_s, db_s, h_s, dxa, dxo,
-    t_sem, w_sem, dwp_sem, misc_sem, dwo_sem, out_sem,
+    xv, dv, dwa, dxp, sums, flip, dn, da_s, db_s, h_s, dxa, dxo,
+    t_sem, misc_sem, dwo_sem, out_sem,
 ):
     row = lax.axis_index("row")
     f = lax.axis_index("fsdp")
@@ -364,41 +354,24 @@
         src, dst = ((x_hbm, xv), (dy_hbm, dv))[which]
         return pltpu.make_async_copy(src.at[:, pl.ds(TA + 512 * t, 512)], dst.at[:, pl.ds(512 * t, 512)], t_sem.at[2 * t + which])
 
-    def w_load(g, i):
-        rows = pl.ds(768 * g, 768)
-        return pltpu.make_async_copy(w_hbm.at[i, rows, :], w.at[i, rows, :], w_sem.at[3 * g + i])
-
-    def dwp_load(g):
-        at = pl.ds(768 * g, 768)
-        return pltpu.make_async_copy(dwp_hbm.at[:, :, at], dwa.at[:, :, at], dwp_sem.at[g])
-
     sum_load = pltpu.make_async_copy(sum_hbm, sums, misc_sem.at[0])
     dxp_load = pltpu.make_async_copy(dxp_hbm, dxp, misc_sem.at[1])
     dxp_store = pltpu.make_async_copy(dxp, dx_out.at[:, pl.ds(0, TA)], misc_sem.at[2])
     dx_store = pltpu.make_async_copy(dxo, dx_out.at[:, pl.ds(TA, TB)], out_sem.at[0])
     dn_store = pltpu.make_async_copy(dn, dn_out, out_sem.at[1])
 
-    w_load(0, 0).start()
     t_load(0, 0).start()
-    w_load(0, 1).start()
-    w_load(0, 2).start()
     t_load(0, 1).start()
     t_load(1, 0).start()
     t_load(1, 1).start()
     sum_load.start()
-    dwp_load(0).start()
-    for i in range(3):
-        w_load(1, i).start()
     dxp_load.start()
-    dwp_load(1).start()
-    for i in range(3):
-        w_load(0, i).wait()
 
     def dw_copy(k):
         at = pl.ds(pl.multiple_of(128 * granule[k], 128), 128)
         return pltpu.make_async_copy(dwa.at[:, :, pl.ds(128 * k, 128)], dw_out.at[:, :, at], dwo_sem.at[k])
 
-    def tile_step(g, t, between):
+    def tile_step(g, t, first):
         rows = pl.ds(768 * g, 768)
         at = pl.ds(pl.multiple_of(t * 512, 512), 512)
         xt, dyt = xv[:, at], dv[:, at]
@@ -409,16 +382,13 @@
             dxa[:, at] = dx
         else:
             dxo[:, at] = (dxa[:, at] + dx).astype(BF)
-        if between is not None:
-            between()
-        dwa[0, :, rows] += dot(xt, da, NT)
-        dwa[1, :, rows] += dot(xt, db, NT)
-        dwa[2, :, rows] += dot(dyt, h, NT)
+        for i, (lhs, rhs) in enumerate(((xt, da), (xt, db), (dyt, h))):
+            dwa[i, :, rows] = (dwp if first else dwa)[i, :, rows] + dot(lhs, rhs, NT)
 
     for t in range(2):
         for which in range(2):
             t_load(t, which).wait()
-        tile_step(0, t, dwp_load(0).wait if t == 0 else None)
+        tile_step(0, t, t == 0)
     for k in range(6):
         dw_copy(k).start()
     sum_load.wait()
@@ -426,15 +396,11 @@
         flip[...] = jnp.transpose(sums[pl.ds(576 * i, 576), :].astype(F32))
         dn[i] = flip[pl.ds(pl.multiple_of(64 * c, 64), 192), :]
     dn_store.start()
-    for i in range(3):
-        w_load(1, i).wait()
     dxp_load.wait()
     dxp_store.start()
-    dwp_load(1).wait()
-
-    @pl.loop(0, TB // 512)
-    def _(t):
-        tile_step(1, t, None)
+
+    for t in range(TB // 512):
+        tile_step(1, t, t == 0)
 
     for k in range(6, 12):
         dw_copy(k).start()
@@ -453,32 +419,34 @@
     shape = jax.ShapeDtypeStruct
     w_all, dw_part, dx_part, sums = pl.pallas_call(
         kernel_a,
-        out_shape=(shape((3, H, D), BF), shape((3, D, H), F32), shape((D, TA), BF), shape((12, CH, 256), BF)),
+        out_shape=(vm((3, H, D), BF), vm((3, D, H), F32), pltpu.HBM((D, TA), BF), pltpu.HBM((12, CH, 256), BF)),
         in_specs=[ANY] * 6,
-        out_specs=(ANY,) * 4,
+        out_specs=(VM, VM, ANY, ANY),
         scratch_shapes=[
-            vm((D, TA), BF), vm((D, TA), BF), vm((3, H, D), BF), vm((768, 1024), BF), vm((768, 1024), BF), vm((768, 1024), BF),
-            vm((D, TA), F32), vm((2, D, 512), BF), vm((3, D, H), F32),
+            vm((D, TA), BF), vm((D, TA), BF), vm((768, 1024), BF), vm((768, 1024), BF), vm((768, 1024), BF),
+            vm((D, TA), F32), vm((2, D, 512), BF),
             vm((6, CH, H), F32), vm((6, CH, H), BF), vm((6, CH, H), BF), vm((6, CH, H), BF), vm((3, CH, H), BF),
             vm((3, CH, 2 * BLK), BF), vm((3, CH, 2 * BLK), BF), vm((3, CH, BLK), BF), vm((6, CH, BLK), BF), vm((6, CH, 256), BF),
             dma((TA // 512,)), dma((6,)), dma((14,)), dma((14,)), dma((6,)), dma((6,)), dma((6,)), dma((3,)), dma((3,)),
             dma((3, 2)), dma((3, 2)), dma((3,)), dma((3,)), dma((3,)), dma((3,)), dma, dma, dma((2,)), dma((3,)), dma((3,)),
         ],
-        compiler_params=pltpu.CompilerParams(collective_id=0, has_side_effects=True, vmem_limit_bytes=VMEM_LIMIT),
+        compiler_params=pltpu.CompilerParams(collective_id=0, has_side_effects=True, vmem_limit_bytes=VMEM_A),
         name="gather_reduce_backward",
     )(x_t, dy_t, gate_shard.T, up_shard.T, down_shard, g_part.reshape(3 * D, H))
+    w_all = pltpu.with_memory_space_constraint(w_all, pltpu.VMEM)
+    dw_part = pltpu.with_memory_space_constraint(dw_part, pltpu.VMEM)
     dx_t, dw_local, dn_t = pl.pallas_call(
         kernel_b,
         out_shape=(shape((D, T), BF), shape((3, D, H), F32), shape((3, 192, D), F32)),
-        in_specs=[ANY] * 6,
+        in_specs=[ANY, ANY, VM, VM, ANY, ANY],
         out_specs=(ANY,) * 3,
         scratch_shapes=[
-            vm((D, TB), BF), vm((D, TB), BF), vm((3, H, D), BF), vm((3, D, H), F32), vm((D, TA), BF), vm((3 * D, 256), BF),
+            vm((D, TB), BF), vm((D, TB), BF), vm((3, D, H), F32), vm((D, TA), BF), vm((3 * D, 256), BF),
             vm((256, D), F32), vm((3, 192, D), F32), vm((768, 512), BF), vm((768, 512), BF), vm((768, 512), BF),
             vm((D, TB), F32), vm((D, TB), BF),
-            dma((TB // 256,)), dma((6,)), dma((2,)), dma((3,)), dma((12,)), dma((2,)),
+            dma((TB // 256,)), dma((3,)), dma((12,)), dma((2,)),
         ],
-        compiler_params=pltpu.CompilerParams(vmem_limit_bytes=VMEM_LIMIT),
+        compiler_params=pltpu.CompilerParams(vmem_limit_bytes=VMEM_B),
         name="finish_backward",
     )(x_t, dy_t, w_all, dw_part, dx_part, sums.reshape(3 * D, 256))
     return dx_t.T, jnp.swapaxes(dn_t, 1, 2), dw_local[None]

time: 96 us -> 92.8 us (0.967)
  Pallas kernels: 95 us -> 91.9 us
    pallas_call x1, Pallas kernels: 70.2 us -> 68.3 us  [per_device(): pl.pallas_call(kernel_a, out_shape=(vm((3, H, D), BF), vm((3, D, H), F32)...]
    pallas_call x1, Pallas kernels: 24.8 us -> 23.6 us  [per_device(): pl.pallas_call(kernel_b, out_shape=(shape((D, T), BF), shape((3, D, H), F...]
where the time goes in v3:
time: 92.8 us; the launch traced here: 92.7 us
  Pallas kernels  91.9 us (99%)
    pallas_call x1, Pallas kernels, per_device(): pl.pallas_call(kernel_a, out_shape=(vm((3, H, D), BF), vm((3, D, H), F32)...  68.3 us
    pallas_call x1, Pallas kernels, per_device(): pl.pallas_call(kernel_b, out_shape=(shape((D, T), BF), shape((3, D, H), F...  23.6 us

profile of v3, /device:TPU:0, one launch (start us, length us, event | category | flops | bytes accessed | tf_op | source)
XLA Modules:
  0.0 92.7 jit_solution(3343757583900195638)
XLA Ops:
  0.6 68.3 %gather_reduce_backward.1 = (bf16[3,1536,576]{2,1,0:T(8,128)(2,1)S(1)}, f32[3,576,1536]{2,1,0:T(8,128)S(1)}, bf16[576,3072]{1,0:T(8,128)(2,1)}, bf16[12,144,256]{2,1,0:T(8,128)(2,1)}) custom-call(bf16[576,4096]{1,0:T(8,128)(2,1)} %bitcast.9, bf16[576,4096]{1,0:T(8,128)(2,1)} %bitcast.11, bf16[192,576]{1,0:T(8,128)(2,1)} %bitcast.15, ...), custom_call_target="tpu_custom_call" | custom-call | tf_op jit(solution)/shard_map/gather_reduce_backward/pallas_call | solution.py:420
  69.0 23.6 %finish_backward.1 = (bf16[576,4096]{1,0:T(8,128)(2,1)}, f32[3,576,1536]{2,1,0:T(8,128)}, f32[3,192,576]{2,1,0:T(8,128)}) custom-call(bf16[576,4096]{1,0:T(8,128)(2,1)} %bitcast.10, bf16[576,4096]{1,0:T(8,128)(2,1)} %bitcast.12, bf16[3,1536,576]{2,1,0:T(8,128)(2,1)S(1)} %get-tuple-element.10.w, f32[3,576,1536]{2,1,0:T(8,128)S(1)} %get-tuple-element.11.dwp, ...), custom_call_target="tpu_custom_call" | custom-call | tf_op jit(solution)/shard_map/finish_backward/pallas_call | solution.py:438

commit v4 on v3

v4 whole, which is shorter than its diff:
```python
import jax
import jax.numpy as jnp
from jax import lax
from jax.experimental import pallas as pl
from jax.experimental.pallas import tpu as pltpu
from jax.sharding import PartitionSpec as P

ALL_AXES = ("dp", "row", "fsdp")
GROUP_AXES = ("row", "fsdp")
MESH = pl.DeviceIdType.MESH
NN = (((1,), (0,)), ((), ()))
NT = (((1,), (1,)), ((), ()))
TN = (((0,), (0,)), ((), ()))
F32 = jnp.float32
BF = jnp.bfloat16
ANY = pl.BlockSpec(memory_space=pl.ANY)
VM = pl.BlockSpec(memory_space=pltpu.VMEM)

D = 576
H = 1536
T = 4096
TA = 3072
TB = T - TA
CH = 144
BLK = 384
VMEM_A = 37 * 2**20
VMEM_B = 37 * 2**20
OWN_OUT, X_OUT, Y_OUT, OWN_MID, X_MID, Y_MID, DIAG = 0, 256, 512, 768, 896, 1024, 1152


def dot(lhs, rhs, dims):
    return lax.dot_general(lhs, rhs, dims, preferred_element_type=F32)


def forward_tile(x, dy, w, rows):
    a = dot(w[0, rows, :], x, NN)
    b = dot(w[1, rows, :], x, NN)
    dh = dot(w[2, rows, :], dy, NN)
    s = jax.nn.sigmoid(a)
    silu = a * s
    h = (silu * b).astype(BF)
    da = (dh * b * s * (1.0 + a * (1.0 - s))).astype(BF)
    db = (dh * silu).astype(BF)
    return h, da, db


def dx_tile(da, db, w, rows):
    return dot(w[0, rows, :], da, TN) + dot(w[1, rows, :], db, TN)


def kernel_a(
    x_hbm, dy_hbm, w1_hbm, w3_hbm, w2_hbm, g_hbm,
    xv, dv, w, dwa, sums, dxo, dx_out, dx2_out,
    da_s, db_s, h_s, dxa,
    stage, part, r0, acc, rz, r1, kept, r2, own,
    in_sem, wl_sem, ws, wr, st_sem, p_s, p_r, z_s, z_r, d1_s, d1_r, d2_s, d2_r, za_s, za_r, f_s, f_r, dxo_sem, dx2_sem,
):
    dp = lax.axis_index("dp")
    row = lax.axis_index("row")
    f = lax.axis_index("fsdp")
    c = lax.rem(f, 2)
    x = f // 2
    fx = lax.rem(f + 2, 4)
    to_core = {"fsdp": f + 1 - 2 * c}
    to_x = {"fsdp": fx}
    to_y = {"row": 1 - row}
    to_z = {"dp": 1 - dp}
    to_xy = {"row": row + (1 - c) * (1 - 2 * row), "fsdp": f + c * (fx - f)}
    to_first = {"row": row + c * (1 - 2 * row), "fsdp": f + (1 - c) * (fx - f)}

    out_l, mid_l = 64 * c, 128 * (1 - c)

    def w_load(n):
        i, mid = n // 2, n % 2
        src = (w1_hbm, w3_hbm, w2_hbm)[i]
        if mid:
            return pltpu.make_async_copy(
                src.at[pl.ds(pl.multiple_of(mid_l, 64), 64), :], w.at[i, pl.ds(pl.multiple_of(OWN_MID + 64 * c, 64), 64), :], wl_sem.at[n]
            )
        return pltpu.make_async_copy(
            src.at[pl.ds(pl.multiple_of(out_l, 64), 128), :], w.at[i, pl.ds(pl.multiple_of(OWN_OUT + 128 * c, 128), 128), :], wl_sem.at[n]
        )

    def g_load(k, side):
        late = k // 3
        half = (1 - late) * (1 - dp) + late * dp
        core = c if side == 0 else 1 - c
        rows = pl.ds(pl.multiple_of(864 * core + 432 * half + CH * (k % 3), 16), CH)
        slot = 2 * (k % 2) + side
        return pltpu.make_async_copy(g_hbm.at[rows, :], stage.at[slot], st_sem.at[slot])

    def t_load(t, which):
        src, dst = ((x_hbm, xv), (dy_hbm, dv))[which]
        cols = pl.ds(pl.multiple_of(t * 1024, 1024), 1024)
        return pltpu.make_async_copy(src.at[:, cols], dst.at[:, cols], in_sem.at[2 * t + which])

    for n in (0, 2, 4, 1, 3, 5):
        w_load(n).start()
    t_load(3, 0).start()
    t_load(3, 1).start()
    for k in range(2):
        g_load(k, 1).start()
        g_load(k, 0).start()

    barrier = pltpu.get_barrier_semaphore()
    for peer in (to_core, to_x, to_y, to_z):
        pl.semaphore_signal(barrier, inc=1, device_id=peer, device_id_type=MESH)
    for i in range(3):
        dwa[i, :, :256] = jnp.zeros((D, 256), F32)
    pl.semaphore_wait(barrier, 4)

    def w_rows(base, size):
        return w.at[:, pl.ds(pl.multiple_of(base, 64), size), :]

    def w_copy(n):
        o, m = 128 * c, 64 * c
        src, dst, size, peer = (
            (OWN_OUT + o, OWN_OUT + o, 128, to_core),
            (OWN_OUT + o, X_OUT + o, 128, to_x),
            (OWN_OUT + o, Y_OUT + o, 128, to_y),
            (OWN_MID + m, OWN_MID + m, 64, to_core),
            (OWN_MID + m, X_MID + m, 64, to_x),
            (OWN_MID + m, Y_MID + m, 64, to_y),
            (X_OUT + o, X_OUT + o, 128, to_core),
            (Y_OUT + o, Y_OUT + o, 128, to_core),
            (X_MID + m, X_MID + m, 64, to_core),
            (Y_MID + m, Y_MID + m, 64, to_core),
            (X_OUT + c * (Y_OUT + 128 - X_OUT), DIAG + 256 * c, 128, to_xy),
            (X_MID + c * (Y_MID + 64 - X_MID), DIAG + 128 + m, 64, to_xy),
            (DIAG + 256 * c, DIAG + 256 * c, 128, to_core),
            (DIAG + 128 + m, DIAG + 128 + m, 64, to_core),
        )[n]
        return pltpu.make_async_remote_copy(
            src_ref=w_rows(src, size), dst_ref=w_rows(dst, size), send_sem=ws.at[n], recv_sem=wr.at[n], device_id=peer, device_id_type=MESH
        )

    def w_send(*ns):
        for n in ns:
            w_copy(n).start()

    def w_arrived(*ns):
        for n in ns:
            w_copy(n).wait_recv()

    def remote(src, dst, s, r, peer):
        return pltpu.make_async_remote_copy(src_ref=src, dst_ref=dst, send_sem=s, recv_sem=r, device_id=peer, device_id_type=MESH)

    def p_copy(k):
        return remote(part.at[k], r0.at[k], p_s.at[k], p_r.at[k], to_core)

    def z_copy(k):
        return remote(acc.at[k], rz.at[k], z_s.at[k], z_r.at[k], to_z)

    def cols(q):
        return pl.ds(pl.multiple_of(q * BLK, BLK), BLK)

    def q_of(j, mine):
        on_x = 2 * j + (x if mine else 1 - x)
        on_y = 2 * (row if mine else 1 - row) + j
        return (1 - c) * on_x + c * on_y

    def d1_copy(k, j):
        return remote(acc.at[3 + k, :, cols(q_of(j, False))], r1.at[k, :, pl.ds(BLK * j, BLK)], d1_s.at[k, j], d1_r.at[k, j], to_first)

    m = (1 - c) * row + c * x

    def d2_copy(k):
        return remote(kept.at[k, :, cols(1 - m)], r2.at[k], d2_s.at[k], d2_r.at[k], to_xy)

    def za_copy(k):
        return remote(own.at[3 * dp + k], own.at[3 * dp + k], za_s.at[k], za_r.at[k], to_z)

    def za_arrival(k):
        return remote(own.at[3 * dp + k], own.at[3 * (1 - dp) + k], za_s.at[k], za_r.at[k], to_z)

    def lanes(core):
        return pl.ds(pl.multiple_of(128 * core, 128), 256)

    f_copy = remote(own.at[:, :, lanes(1 - c)], sums.at[pl.ds(6 * c, 6)], f_s, f_r, to_core)
    f_arrival = remote(own.at[:, :, lanes(1 - c)], sums.at[pl.ds(6 * (1 - c), 6)], f_s, f_r, to_core)

    def convert(k):
        slot = 2 * (k % 2)
        part[k] = stage[slot + 1].astype(BF)
        acc[k] = stage[slot].astype(BF)

    def g_loaded(k):
        g_load(k, 1).wait()
        g_load(k, 0).wait()

    def z_step(k):
        p_copy(3 + k).wait_recv()
        z_copy(k).wait_recv()
        acc[3 + k] = acc[3 + k] + r0[3 + k] + rz[k]

    def d1_send(k):
        d1_copy(k, 0).start()
        d1_copy(k, 1).start()

    def d1_step(k):
        for j in range(2):
            d1_copy(k, j).wait_recv()
        for j in range(2):
            at = pl.ds(BLK * j, BLK)
            kept[k, :, at] = acc[3 + k, :, cols(q_of(j, True))] + r1[k, :, at]

    def d2_step(k):
        d2_copy(k).wait_recv()
        own[3 * dp + k] = kept[k, :, cols(m)] + r2[k]

    def dx_copy(t, size):
        at = pl.ds(pl.multiple_of(t * size, size), size)
        return pltpu.make_async_copy(dxo.at[lax.rem(t, 2)], dx_out.at[:, at], dxo_sem.at[lax.rem(t, 2)])

    dx2_copy = pltpu.make_async_copy(dxa.at[:, pl.ds(2048, TB)], dx2_out, dx2_sem)

    def tile_step(base, size, t, tile, put):
        rows = pl.ds(base, size)
        at = pl.ds(pl.multiple_of(t * tile, tile), tile)
        xt, dyt = xv[:, at], dv[:, at]
        h_s[:size, :tile], da_s[:size, :tile], db_s[:size, :tile] = forward_tile(xt, dyt, w, rows)
        h, da, db = h_s[:size, :tile], da_s[:size, :tile], db_s[:size, :tile]
        put(at, dx_tile(da, db, w, rows))
        dwa[0, :, rows] += dot(xt, da, NT)
        dwa[1, :, rows] += dot(xt, db, NT)
        dwa[2, :, rows] += dot(dyt, h, NT)

    for n in (0, 2, 4):
        w_load(n).wait()
    w_send(0, 1, 2)
    for n in (1, 3, 5):
        w_load(n).wait()
    w_send(3, 4, 5)
    w_arrived(0)

    def add_partner(k):
        p_copy(k).wait_recv()
        acc[k] = acc[k] + r0[k]

    @pl.loop(0, T // 1024)
    def _(t):
        @pl.when(t < 3)
        def _():
            t_load(t, 0).start()
            t_load(t, 1).start()

        @pl.when(t == 1)
        def _():
            dx2_copy.start()

        @pl.when(t > 1)
        def _():
            add_partner(t - 2)

        @pl.when(t > 0)
        def _():
            p_copy(t - 1).start()
            g_load(t + 1, 1).start()
            g_load(t + 1, 0).start()

        @pl.when(t > 1)
        def _():
            z_copy(t - 2).start()

        @pl.when(t == 3)
        def _():
            dx2_copy.wait()

        tt = lax.rem(t + 3, 4)
        t_load(tt, 0).wait()
        t_load(tt, 1).wait()
        g_loaded(t)
        convert(t)

        def put(at, dx):
            dxa[:, pl.ds(pl.multiple_of(1024 * lax.rem(t + 2, 3), 1024), 1024)] = dx

        tile_step(0, 256, tt, 1024, put)

    p_copy(3).start()
    w_arrived(1, 2)
    w_send(6, 7, 10)
    g_load(5, 1).start()
    g_load(5, 0).start()
    g_loaded(4)
    convert(4)
    add_partner(2)
    for i in range(3):
        dwa[i, :, 256:] = jnp.zeros((D, H - 256), F32)
    z_copy(2).start()
    p_copy(4).start()
    w_arrived(6, 7)

    def add_dx(at, dx):
        dxa[:, at] += dx

    @pl.loop(0, TA // 1024)
    def _(t):
        @pl.when(t == 1)
        def _():
            w_arrived(3, 4, 5)
            w_send(8, 9, 11)
            g_loaded(5)
            convert(5)
            z_step(0)
            p_copy(5).start()
            d1_send(0)

        @pl.when(t == 2)
        def _():
            w_arrived(10, 11)
            w_send(12, 13)
            d1_step(0)
            d2_copy(0).start()

        tile_step(256, 512, t, 1024, add_dx)

    d2_step(0)
    z_step(1)
    za_copy(0).start()
    d1_send(1)
    w_arrived(8, 9, 12, 13)

    def at_1():
        d1_step(1)
        d2_copy(1).start()

    def at_2():
        d2_step(1)
        z_step(2)
        za_copy(1).start()
        d1_send(2)

    def at_3():
        d1_step(2)
        d2_copy(2).start()

    def at_4():
        d2_step(2)
        za_copy(2).start()

    def at_5():
        for k in range(3):
            za_arrival(k).wait_recv()
        f_copy.start()
        sums[pl.ds(6 * c, 6)] = own[:, :, lanes(c)]

    @pl.loop(0, TA // 512)
    def _(t):
        for i, step in ((1, at_1), (2, at_2), (3, at_3), (4, at_4), (5, at_5)):
            pl.when(t == i)(step)

        @pl.when(t >= 2)
        def _():
            dx_copy(t - 2, 512).wait()

        def put(at, dx):
            dxo[lax.rem(t, 2)] = (dxa[:, at] + dx).astype(BF)

        tile_step(768, 768, t, 512, put)

        @pl.when(t < TA // 512 - 2)
        def _():
            dx_copy(t, 512).start()

    f_arrival.wait_recv()
    for n in range(14):
        w_copy(n).wait_send()
    for k in range(6):
        p_copy(k).wait_send()
    for k in range(3):
        z_copy(k).wait_send()
        d1_copy(k, 0).wait_send()
        d1_copy(k, 1).wait_send()
        d2_copy(k).wait_send()
        za_copy(k).wait_send()
    f_copy.wait_send()


def kernel_b(
    xv, dv, w, dwp, sums, dxo_a, dxp_hbm, dx2_hbm,
    dx_out, dw_out, dn_out,
    dwa, dxp, dx2, flip, dn, da_s, db_s, h_s, dxa, dxo,
    misc_sem, dw_sem, last_sem,
):
    row = lax.axis_index("row")
    f = lax.axis_index("fsdp")
    c = lax.rem(f, 2)
    x = f // 2
    q_own, q_x, q_y, q_d = 2 * row + x, 2 * row + 1 - x, 2 * (1 - row) + x, 2 * (1 - row) + 1 - x
    granule = [3 * q + j for q, j in (
        (q_own, 0), (q_own, 2), (q_x, 0), (q_x, 2), (q_y, 0), (q_y, 2), (q_own, 1), (q_x, 1), (q_y, 1), (q_d, 0), (q_d, 1), (q_d, 2)
    )]

    dxp_load = pltpu.make_async_copy(dxp_hbm, dxp, misc_sem.at[0])
    dxp_store = pltpu.make_async_copy(dxp, dx_out.at[:, pl.ds(0, TA - 1024)], misc_sem.at[1])
    dx2_load = pltpu.make_async_copy(dx2_hbm, dx2, misc_sem.at[2])
    dx_store = pltpu.make_async_copy(dxo, dx_out.at[:, pl.ds(TA, TB)], misc_sem.at[3])
    dn_store = pltpu.make_async_copy(dn, dn_out, misc_sem.at[4])

    def tail_store(i):
        return pltpu.make_async_copy(dxo_a.at[i], dx_out.at[:, pl.ds(TA - 1024 + 512 * i, 512)], misc_sem.at[5 + i])

    def place(k):
        return pl.ds(pl.multiple_of(128 * granule[k], 128), 128)

    def dw_copy(k):
        src = dwp if k < 2 else dwa
        return pltpu.make_async_copy(src.at[:, :, pl.ds(128 * k, 128)], dw_out.at[:, :, place(k)], dw_sem.at[k])

    def last_copy(i, k):
        return pltpu.make_async_copy(dwa.at[i, :, pl.ds(128 * k, 128)], dw_out.at[i, :, place(k)], last_sem.at[i, k - 2])

    for k in range(2):
        dw_copy(k).start()
    dxp_load.start()
    dx2_load.start()
    tail_store(0).start()
    tail_store(1).start()

    rows = pl.ds(768, 768)
    for t in range(2):
        mine, at = pl.ds(TA + 512 * t, 512), pl.ds(512 * t, 512)
        xt, dyt = xv[:, mine], dv[:, mine]
        h_s[:, :512], da_s[:, :512], db_s[:, :512] = forward_tile(xt, dyt, w, rows)
        h, da, db = h_s[:, :512], da_s[:, :512], db_s[:, :512]
        dxa[:, at] = dx_tile(da, db, w, rows)
        for i, (lhs, rhs) in enumerate(((xt, da), (xt, db), (dyt, h))):
            dwa[i, :, rows] = (dwp if t == 0 else dwa)[i, :, rows] + dot(lhs, rhs, NT)
    for k in range(6, 12):
        dw_copy(k).start()
    dxp_load.wait()
    dxp_store.start()
    dx2_load.wait()

    rows = pl.ds(256, 512)
    xt, dyt = xv[:, TA:], dv[:, TA:]
    for i in range(3):
        flip[i] = jnp.transpose(sums[4 * i : 4 * i + 4].reshape(D, 256).astype(F32))
        dn[i] = flip[i, pl.ds(pl.multiple_of(64 * c, 64), 192), :]
    h_s[:512], da_s[:512], db_s[:512] = forward_tile(xt, dyt, w, rows)
    h, da, db = h_s[:512], da_s[:512], db_s[:512]
    dxo[...] = (dxa[...] + dx2[...] + dx_tile(da, db, w, rows)).astype(BF)
    dx_store.start()
    dn_store.start()
    for i, (lhs, rhs) in enumerate(((xt, da), (xt, db), (dyt, h))):
        dwa[i, :, rows] = dwp[i, :, rows] + dot(lhs, rhs, NT)
        for k in range(2, 6):
            last_copy(i, k).start()

    for k in (0, 1, 6, 7, 8, 9, 10, 11):
        dw_copy(k).wait()
    dxp_store.wait()
    tail_store(0).wait()
    tail_store(1).wait()
    dx_store.wait()
    dn_store.wait()
    for i in range(3):
        for k in range(2, 6):
            last_copy(i, k).wait()


def per_device(x_blk, dy_blk, gate_shard, up_shard, down_shard, g_part):
    dma = pltpu.SemaphoreType.DMA
    vm, hbm = pltpu.VMEM, pltpu.HBM
    shape = jax.ShapeDtypeStruct
    *in_vmem, dx_part, dx2_part = pl.pallas_call(
        kernel_a,
        out_shape=(
            vm((D, T), BF), vm((D, T), BF), vm((3, H, D), BF), vm((3, D, H), F32), vm((12, CH, 256), BF), vm((2, D, 512), BF), hbm((D, TA - 1024), BF), hbm((D, TB), F32)
        ),
        in_specs=[ANY] * 6,
        out_specs=(VM,) * 6 + (ANY,) * 2,
        scratch_shapes=[
            vm((768, 1024), BF), vm((768, 1024), BF), vm((768, 1024), BF), vm((D, TA), F32),
            vm((4, CH, H), F32), vm((6, CH, H), BF), vm((6, CH, H), BF), vm((6, CH, H), BF), vm((3, CH, H), BF),
            vm((3, CH, 2 * BLK), BF), vm((3, CH, 2 * BLK), BF), vm((3, CH, BLK), BF), vm((6, CH, BLK), BF),
            dma((T // 512,)), dma((6,)), dma((14,)), dma((14,)), dma((4,)), dma((6,)), dma((6,)), dma((3,)), dma((3,)),
            dma((3, 2)), dma((3, 2)), dma((3,)), dma((3,)), dma((3,)), dma((3,)), dma, dma, dma((2,)), dma,
        ],
        compiler_params=pltpu.CompilerParams(collective_id=0, has_side_effects=True, vmem_limit_bytes=VMEM_A),
        name="gather_reduce_backward",
    )(x_blk.T, dy_blk.T, gate_shard.T, up_shard.T, down_shard, g_part.reshape(3 * D, H))
    in_vmem = [pltpu.with_memory_space_constraint(v, pltpu.VMEM) for v in in_vmem]
    dx_t, dw_local, dn_t = pl.pallas_call(
        kernel_b,
        out_shape=(shape((D, T), BF), shape((3, D, H), F32), shape((3, 192, D), F32)),
        in_specs=[VM] * 6 + [ANY] * 2,
        out_specs=(ANY,) * 3,
        scratch_shapes=[
            vm((3, D, H), F32), vm((D, TA - 1024), BF), vm((D, TB), F32), vm((3, 256, D), F32), vm((3, 192, D), F32),
            vm((768, TB), BF), vm((768, TB), BF), vm((768, TB), BF), vm((D, TB), F32), vm((D, TB), BF),
            dma((7,)), dma((12,)), dma((3, 4)),
        ],
        compiler_params=pltpu.CompilerParams(vmem_limit_bytes=VMEM_B),
        name="finish_backward",
    )(*in_vmem, dx_part, dx2_part)
    return dx_t.T, jnp.swapaxes(dn_t, 1, 2), dw_local[None]


def solution(mesh):
    return jax.shard_map(
        per_device,
        mesh=mesh,
        in_specs=(P(ALL_AXES, None), P(ALL_AXES, None), P(None, GROUP_AXES), P(None, GROUP_AXES), P(GROUP_AXES, None), P(ALL_AXES, None, None, None)),
        out_specs=(P(ALL_AXES, None), P(None, None, GROUP_AXES), P(ALL_AXES, None, None, None)),
        check_vma=False,
    )
```

time: 92.8 us -> 88.4 us (0.953)
  Pallas kernels: 91.9 us -> 87.5 us
    pallas_call x1, Pallas kernels: 23.6 us -> 17.8 us  [per_device(): pl.pallas_call(kernel_b, out_shape=(shape((D, T), BF), shape((3, D, H), F...]
    pallas_call x1, Pallas kernels: 68.3 us -> 69.8 us  [per_device(): pl.pallas_call(kernel_a, out_shape=(vm((D, T), BF), vm((D, T), BF), vm((3...]
where the time goes in v4:
time: 88.4 us; the launch traced here: 88.3 us
  Pallas kernels  87.5 us (99%)
    pallas_call x1, Pallas kernels, per_device(): pl.pallas_call(kernel_a, out_shape=(vm((D, T), BF), vm((D, T), BF), vm((3...  69.8 us
    pallas_call x1, Pallas kernels, per_device(): pl.pallas_call(kernel_b, out_shape=(shape((D, T), BF), shape((3, D, H), F...  17.8 us

profile of v4, /device:TPU:0, one launch (start us, length us, event | category | flops | bytes accessed | tf_op | source)
XLA Modules:
  0.0 88.3 jit_solution(771775637338545993)
XLA Ops:
  0.6 69.8 %gather_reduce_backward.1 = (bf16[576,4096]{1,0:T(8,128)(2,1)S(1)}, bf16[576,4096]{1,0:T(8,128)(2,1)S(1)}, bf16[3,1536,576]{2,1,0:T(8,128)(2,1)S(1)}, f32[3,576,...) custom-call(bf16[576,4096]{1,0:T(8,128)(2,1)} %bitcast.9, ...), custom_call_target="tpu_custom_call" | custom-call | tf_op jit(solution)/shard_map/gather_reduce_backward/pallas_call | solution.py:467
  70.4 17.8 %finish_backward.1 = (bf16[576,4096]{1,0:T(8,128)(2,1)}, f32[3,576,1536]{2,1,0:T(8,128)}, f32[3,192,576]{2,1,0:T(8,128)}) custom-call(bf16[576,4096]{1,0:T(8,128)(2,1)S(1)} %get-tuple-element.14.xv, bf16[576,4096]{1,0:T(8,128)(2,1)S(1)} %get-tuple-element.15.dv, bf16[3,1536,576]{2,1,0:T(8,128)(2,1)S(1)} %get-tuple-element.16.w, ...), custom_call_target="tpu_custom_call" | custom-call | tf_op jit(solution)/shard_map/finish_backward/pallas_call | solution.py:485

commit v5 on v4

--- a/solution.py
+++ b/solution.py
@@ -106,7 +106,7 @@
     for peer in (to_core, to_x, to_y, to_z):
         pl.semaphore_signal(barrier, inc=1, device_id=peer, device_id_type=MESH)
     for i in range(3):
-        dwa[i, :, :256] = jnp.zeros((D, 256), F32)
+        dwa[i] = jnp.zeros((D, H), F32)
     pl.semaphore_wait(barrier, 4)
 
     def w_rows(base, size):
@@ -214,13 +214,19 @@
 
     dx2_copy = pltpu.make_async_copy(dxa.at[:, pl.ds(2048, TB)], dx2_out, dx2_sem)
 
-    def tile_step(base, size, t, tile, put):
+    def tile_step(base, size, t, tile, put, parts=1):
         rows = pl.ds(base, size)
         at = pl.ds(pl.multiple_of(t * tile, tile), tile)
+        sub = tile // parts
+        for j in range(parts):
+            ats = pl.ds(pl.multiple_of(t * tile + j * sub, sub), sub)
+            cut = slice(j * sub, (j + 1) * sub)
+            h_s[:size, cut], da_s[:size, cut], db_s[:size, cut] = forward_tile(xv[:, ats], dv[:, ats], w, rows)
+        for j in range(parts):
+            cut = slice(j * sub, (j + 1) * sub)
+            put(j * sub, sub, dx_tile(da_s[:size, cut], db_s[:size, cut], w, rows))
         xt, dyt = xv[:, at], dv[:, at]
-        h_s[:size, :tile], da_s[:size, :tile], db_s[:size, :tile] = forward_tile(xt, dyt, w, rows)
         h, da, db = h_s[:size, :tile], da_s[:size, :tile], db_s[:size, :tile]
-        put(at, dx_tile(da, db, w, rows))
         dwa[0, :, rows] += dot(xt, da, NT)
         dwa[1, :, rows] += dot(xt, db, NT)
         dwa[2, :, rows] += dot(dyt, h, NT)
@@ -231,6 +237,11 @@
     for n in (1, 3, 5):
         w_load(n).wait()
     w_send(3, 4, 5)
+    g_loaded(0)
+    convert(0)
+    g_load(2, 1).start()
+    g_load(2, 0).start()
+    p_copy(0).start()
     w_arrived(0)
 
     def add_partner(k):
@@ -248,51 +259,35 @@
         def _():
             dx2_copy.start()
 
-        @pl.when(t > 1)
-        def _():
-            add_partner(t - 2)
-
         @pl.when(t > 0)
         def _():
-            p_copy(t - 1).start()
-            g_load(t + 1, 1).start()
-            g_load(t + 1, 0).start()
-
-        @pl.when(t > 1)
-        def _():
-            z_copy(t - 2).start()
+            add_partner(t - 1)
+            p_copy(t).start()
+            g_load(t + 2, 1).start()
+            g_load(t + 2, 0).start()
+            z_copy(t - 1).start()
 
         @pl.when(t == 3)
         def _():
             dx2_copy.wait()
+            w_arrived(1, 2)
+            w_send(6, 7, 10)
 
         tt = lax.rem(t + 3, 4)
         t_load(tt, 0).wait()
         t_load(tt, 1).wait()
-        g_loaded(t)
-        convert(t)
-
-        def put(at, dx):
-            dxa[:, pl.ds(pl.multiple_of(1024 * lax.rem(t + 2, 3), 1024), 1024)] = dx
-
-        tile_step(0, 256, tt, 1024, put)
-
-    p_copy(3).start()
-    w_arrived(1, 2)
-    w_send(6, 7, 10)
-    g_load(5, 1).start()
-    g_load(5, 0).start()
-    g_loaded(4)
-    convert(4)
-    add_partner(2)
-    for i in range(3):
-        dwa[i, :, 256:] = jnp.zeros((D, H - 256), F32)
-    z_copy(2).start()
+        g_loaded(t + 1)
+        convert(t + 1)
+
+        def put(off, sub, dx):
+            dxa[:, pl.ds(pl.multiple_of(1024 * lax.rem(t + 2, 3) + off, 256), sub)] = dx
+
+        tile_step(0, 256, tt, 1024, put, 4)
+
     p_copy(4).start()
+    g_loaded(5)
+    convert(5)
     w_arrived(6, 7)
-
-    def add_dx(at, dx):
-        dxa[:, at] += dx
 
     @pl.loop(0, TA // 1024)
     def _(t):
@@ -300,29 +295,30 @@
         def _():
             w_arrived(3, 4, 5)
             w_send(8, 9, 11)
-            g_loaded(5)
-            convert(5)
-            z_step(0)
             p_copy(5).start()
-            d1_send(0)
 
         @pl.when(t == 2)
         def _():
             w_arrived(10, 11)
             w_send(12, 13)
-            d1_step(0)
-            d2_copy(0).start()
-
-        tile_step(256, 512, t, 1024, add_dx)
-
-    d2_step(0)
+            z_step(0)
+            d1_send(0)
+
+        def put(off, sub, dx):
+            dxa[:, pl.ds(pl.multiple_of(1024 * t + off, 256), sub)] += dx
+
+        tile_step(256, 512, t, 1024, put, 4)
+
+    d1_step(0)
     z_step(1)
-    za_copy(0).start()
+    d2_copy(0).start()
     d1_send(1)
     w_arrived(8, 9, 12, 13)
 
     def at_1():
+        d2_step(0)
         d1_step(1)
+        za_copy(0).start()
         d2_copy(1).start()
 
     def at_2():
@@ -354,8 +350,8 @@
         def _():
             dx_copy(t - 2, 512).wait()
 
-        def put(at, dx):
-            dxo[lax.rem(t, 2)] = (dxa[:, at] + dx).astype(BF)
+        def put(off, sub, dx):
+            dxo[lax.rem(t, 2)] = (dxa[:, pl.ds(pl.multiple_of(512 * t, 512), 512)] + dx).astype(BF)
 
         tile_step(768, 768, t, 512, put)
 
@@ -438,9 +434,12 @@
     for i in range(3):
         flip[i] = jnp.transpose(sums[4 * i : 4 * i + 4].reshape(D, 256).astype(F32))
         dn[i] = flip[i, pl.ds(pl.multiple_of(64 * c, 64), 192), :]
-    h_s[:512], da_s[:512], db_s[:512] = forward_tile(xt, dyt, w, rows)
+    cuts = [slice(j, j + 256) for j in range(0, TB, 256)]
+    for cut in cuts:
+        h_s[:512, cut], da_s[:512, cut], db_s[:512, cut] = forward_tile(xt[:, cut], dyt[:, cut], w, rows)
+    for cut in cuts:
+        dxo[:, cut] = (dxa[:, cut] + dx2[:, cut] + dx_tile(da_s[:512, cut], db_s[:512, cut], w, rows)).astype(BF)
     h, da, db = h_s[:512], da_s[:512], db_s[:512]
-    dxo[...] = (dxa[...] + dx2[...] + dx_tile(da, db, w, rows)).astype(BF)
     dx_store.start()
     dn_store.start()
     for i, (lhs, rhs) in enumerate(((xt, da), (xt, db), (dyt, h))):

time: 88.4 us -> 86.4 us (0.977)
  Pallas kernels: 87.5 us -> 85.5 us
    pallas_call x1, Pallas kernels: 69.8 us -> 67.8 us  [per_device(): pl.pallas_call(kernel_a, out_shape=(vm((D, T), BF), vm((D, T), BF), vm((3...]
where the time goes in v5:
time: 86.4 us; the launch traced here: 86.3 us
  Pallas kernels  85.5 us (99%)
    pallas_call x1, Pallas kernels, per_device(): pl.pallas_call(kernel_a, out_shape=(vm((D, T), BF), vm((D, T), BF), vm((3...  67.8 us
    pallas_call x1, Pallas kernels, per_device(): pl.pallas_call(kernel_b, out_shape=(shape((D, T), BF), shape((3, D, H), F...  17.8 us

profile of v5, /device:TPU:0, one launch (start us, length us, event | category | flops | bytes accessed | tf_op | source)
XLA Modules:
  0.0 86.3 jit_solution(1256118191077553494)
XLA Ops:
  0.6 67.8 %gather_reduce_backward.1 = (bf16[576,4096]{1,0:T(8,128)(2,1)S(1)}, bf16[576,4096]{1,0:T(8,128)(2,1)S(1)}, bf16[3,1536,576]{2,1,0:T(8,128)(2,1)S(1)}, f32[3,576,...) custom-call(bf16[576,4096]{1,0:T(8,128)(2,1)} %bitcast.9, ...), custom_call_target="tpu_custom_call" | custom-call | tf_op jit(solution)/shard_map/gather_reduce_backward/pallas_call | solution.py:466
  68.4 17.8 %finish_backward.1 = (bf16[576,4096]{1,0:T(8,128)(2,1)}, f32[3,576,1536]{2,1,0:T(8,128)}, f32[3,192,576]{2,1,0:T(8,128)}) custom-call(bf16[576,4096]{1,0:T(8,128)(2,1)S(1)} %get-tuple-element.14.xv, bf16[576,4096]{1,0:T(8,128)(2,1)S(1)} %get-tuple-element.15.dv, bf16[3,1536,576]{2,1,0:T(8,128)(2,1)S(1)} %get-tuple-element.16.w, ...), custom_call_target="tpu_custom_call" | custom-call | tf_op jit(solution)/shard_map/finish_backward/pallas_call | solution.py:484

commit v6 on v5

--- a/solution.py
+++ b/solution.py
@@ -317,18 +317,18 @@
 
     def at_1():
         d2_step(0)
+        z_step(2)
+        za_copy(0).start()
+        d1_send(2)
+
+    def at_2():
         d1_step(1)
-        za_copy(0).start()
         d2_copy(1).start()
 
-    def at_2():
+    def at_3():
         d2_step(1)
-        z_step(2)
+        d1_step(2)
         za_copy(1).start()
-        d1_send(2)
-
-    def at_3():
-        d1_step(2)
         d2_copy(2).start()
 
     def at_4():

time: 86.4 us -> 86 us (level)
  no operation moved by 1% of the time
where the time goes in v6:
time: 86 us; the launch traced here: 85.9 us
  Pallas kernels  85.1 us (99%)
    pallas_call x1, Pallas kernels, per_device(): pl.pallas_call(kernel_a, out_shape=(vm((D, T), BF), vm((D, T), BF), vm((3...  67.3 us
    pallas_call x1, Pallas kernels, per_device(): pl.pallas_call(kernel_b, out_shape=(shape((D, T), BF), shape((3, D, H), F...  17.8 us

profile of v6, /device:TPU:0, one launch (start us, length us, event | category | flops | bytes accessed | tf_op | source)
XLA Modules:
  0.0 85.9 jit_solution(7902851015401065592)
XLA Ops:
  0.6 67.3 %gather_reduce_backward.1 = (bf16[576,4096]{1,0:T(8,128)(2,1)S(1)}, bf16[576,4096]{1,0:T(8,128)(2,1)S(1)}, bf16[3,1536,576]{2,1,0:T(8,128)(2,1)S(1)}, f32[3,576,...) custom-call(bf16[576,4096]{1,0:T(8,128)(2,1)} %bitcast.9, ...), custom_call_target="tpu_custom_call" | custom-call | tf_op jit(solution)/shard_map/gather_reduce_backward/pallas_call | solution.py:466
  68.0 17.8 %finish_backward.1 = (bf16[576,4096]{1,0:T(8,128)(2,1)}, f32[3,576,1536]{2,1,0:T(8,128)}, f32[3,192,576]{2,1,0:T(8,128)}) custom-call(bf16[576,4096]{1,0:T(8,128)(2,1)S(1)} %get-tuple-element.14.xv, bf16[576,4096]{1,0:T(8,128)(2,1)S(1)} %get-tuple-element.15.dv, bf16[3,1536,576]{2,1,0:T(8,128)(2,1)S(1)} %get-tuple-element.16.w, ...), custom_call_target="tpu_custom_call" | custom-call | tf_op jit(solution)/shard_map/finish_backward/pallas_call | solution.py:484

commit v7 on v6

--- a/solution.py
+++ b/solution.py
@@ -105,8 +105,6 @@
     barrier = pltpu.get_barrier_semaphore()
     for peer in (to_core, to_x, to_y, to_z):
         pl.semaphore_signal(barrier, inc=1, device_id=peer, device_id_type=MESH)
-    for i in range(3):
-        dwa[i] = jnp.zeros((D, H), F32)
     pl.semaphore_wait(barrier, 4)
 
     def w_rows(base, size):
@@ -237,6 +235,8 @@
     for n in (1, 3, 5):
         w_load(n).wait()
     w_send(3, 4, 5)
+    for i in range(3):
+        dwa[i] = jnp.zeros((D, H), F32)
     g_loaded(0)
     convert(0)
     g_load(2, 1).start()

time: 86 us -> 86 us (level)
  no operation moved by 1% of the time
where the time goes in v7:
time: 86 us; the launch traced here: 85.9 us
  Pallas kernels  85.1 us (99%)
    pallas_call x1, Pallas kernels, per_device(): pl.pallas_call(kernel_a, out_shape=(vm((D, T), BF), vm((D, T), BF), vm((3...  67.3 us
    pallas_call x1, Pallas kernels, per_device(): pl.pallas_call(kernel_b, out_shape=(shape((D, T), BF), shape((3, D, H), F...  17.8 us

profile of v7, /device:TPU:0, one launch (start us, length us, event | category | flops | bytes accessed | tf_op | source)
XLA Modules:
  0.0 85.9 jit_solution(3822867543038302962)
XLA Ops:
  0.6 67.3 %gather_reduce_backward.1 = (bf16[576,4096]{1,0:T(8,128)(2,1)S(1)}, bf16[576,4096]{1,0:T(8,128)(2,1)S(1)}, bf16[3,1536,576]{2,1,0:T(8,128)(2,1)S(1)}, f32[3,576,...) custom-call(bf16[576,4096]{1,0:T(8,128)(2,1)} %bitcast.9, ...), custom_call_target="tpu_custom_call" | custom-call | tf_op jit(solution)/shard_map/gather_reduce_backward/pallas_call | solution.py:466
  68.0 17.8 %finish_backward.1 = (bf16[576,4096]{1,0:T(8,128)(2,1)}, f32[3,576,1536]{2,1,0:T(8,128)}, f32[3,192,576]{2,1,0:T(8,128)}) custom-call(bf16[576,4096]{1,0:T(8,128)(2,1)S(1)} %get-tuple-element.14.xv, bf16[576,4096]{1,0:T(8,128)(2,1)S(1)} %get-tuple-element.15.dv, bf16[3,1536,576]{2,1,0:T(8,128)(2,1)S(1)} %get-tuple-element.16.w, ...), custom_call_target="tpu_custom_call" | custom-call | tf_op jit(solution)/shard_map/finish_backward/pallas_call | solution.py:484
